TPU v7x, 16 devices: a 4x2x1 block of a 4x4x8 slice. The times are simulated.
16 devices in a mesh: rep: 2 (over y, z), g: 8 (over x, core).
Axes of the slice: x: 4, y: 2, z: 1, core: 2. Of those that a mesh axis runs over, the one named last changes fastest.
The devices are a block of a 4x4x8 slice.
Arguments:
- hidden: bfloat16 [512, 6144], P(('rep', 'g')), parts along dimension 0
- cache_lat: bfloat16 [512, 1024, 512], P(('rep', 'g')), parts along dimension 0
- cache_rope: bfloat16 [512, 1024, 64], P(('rep', 'g')), parts along dimension 0
- seq_lens: int32 [512], P(('rep', 'g')), parts along dimension 0
- gain_attn: bfloat16 [6144], replicated
- w_dq: bfloat16 [6144, 1536], replicated
- gain_q: bfloat16 [1536], replicated
- w_uq: bfloat16 [1536, 64, 128], replicated
- w_qr: bfloat16 [1536, 64, 64], replicated
- w_dkv: bfloat16 [6144, 576], replicated
- gain_kv: bfloat16 [512], replicated
- w_uk: bfloat16 [512, 64, 128], replicated
- w_uv: bfloat16 [512, 64, 128], replicated
- w_o: bfloat16 [8192, 6144], replicated
- gain_mlp: bfloat16 [6144], replicated
- w_gate: bfloat16 [6144, 12288], P(None, 'g')
- w_up: bfloat16 [6144, 12288], P(None, 'g')
- w_down: bfloat16 [12288, 6144], P('g')
Outputs:
- output 1: bfloat16 [512, 6144], P(('rep', 'g')), parts along dimension 0
- output 2: bfloat16 [512, 512], P(('rep', 'g')), parts along dimension 0
- output 3: bfloat16 [512, 64], P(('rep', 'g')), parts along dimension 0
There are 2 independent parts. A program takes and returns all parts, laid end to end along the dimension named above; an argument that names none is the same for every part.
All inputs are finite; a program needn't handle non-finite values.
Results may differ from a plain program's by a relative error of at most 0.0123806.
Values are sent between devices in bfloat16 or wider.
A program may use at most 768 MiB of HBM per device.

v0:
```python
import functools

import jax
import jax.numpy as jnp
from jax import lax
from jax.experimental import pallas as pl
from jax.experimental.pallas import tpu as pltpu
from jax.sharding import PartitionSpec as P


def rms_norm(values, gain_vec):
    mean_sq = jnp.mean(jnp.square(values), axis=-1, keepdims=True)
    return values * lax.rsqrt(mean_sq + 1e-6) * gain_vec.astype(jnp.float32)


def apply_rope(values, positions):
    half_dim = values.shape[-1] // 2
    inv_freq = 10000.0 ** (-jnp.arange(half_dim).astype(jnp.float32) / half_dim)
    angles = positions.astype(jnp.float32)[..., None] * inv_freq
    cos_part = jnp.cos(angles)
    sin_part = jnp.sin(angles)
    first_half = values[..., :half_dim]
    second_half = values[..., half_dim:]
    return jnp.concatenate([first_half * cos_part - second_half * sin_part, first_half * sin_part + second_half * cos_part], axis=-1)


ATT_BLK = 256
ATT_BUF = 4
UV_HEADS = 16


def attn_kernel(lens_ref, q_ref, qr_ref, nl_ref, nr_ref, nl_rows, lat_hbm, rope_hbm, wuv_hbm, o_ref, lat_buf, rope_buf, mix, wuv, lat_sem, rope_sem, wuv_sem):
    rows, heads, kv_dim = q_ref.shape
    cache_len = lat_hbm.shape[1]
    scale = (wuv.shape[2] + qr_ref.shape[2]) ** -0.5
    max_blk = cache_len // ATT_BLK

    def lat_copy(row, blk, slot):
        span = pl.ds(blk * ATT_BLK, ATT_BLK)
        return pltpu.make_async_copy(lat_hbm.at[row, span], lat_buf.at[slot, span], lat_sem.at[slot, blk])

    def rope_copy(row, slot):
        return pltpu.make_async_copy(rope_hbm.at[row], rope_buf.at[slot], rope_sem.at[slot])

    def blocks(row):
        return (lens_ref[row] + ATT_BLK - 1) // ATT_BLK

    def fetch(row, slot):
        count = blocks(row)
        rope_copy(row, slot).start()
        for blk in range(max_blk):
            @pl.when(blk < count)
            def _():
                lat_copy(row, blk, slot).start()

    for row in range(ATT_BUF - 1):
        fetch(row, row)
    wuv_copy = pltpu.make_async_copy(wuv_hbm, wuv, wuv_sem)
    wuv_copy.start()

    own_col = lax.broadcasted_iota(jnp.int32, (heads, rows), 1)
    nl_all = nl_ref[...]
    nr_all = nr_ref[...]
    nt = (((1,), (1,)), ((), ()))

    def one_row(row, carry):
        slot = lax.rem(row, ATT_BUF)
        ahead = row + ATT_BUF - 1

        @pl.when(ahead < rows)
        def _():
            fetch(ahead, lax.rem(ahead, ATT_BUF))

        count = blocks(row)
        length = lens_ref[row]
        rope_copy(row, slot).wait()
        for blk in range(max_blk):
            @pl.when(blk < count)
            def _():
                lat_copy(row, blk, slot).wait()

        for num in range(1, max_blk + 1):
            @pl.when(count == num)
            def _():
                span = num * ATT_BLK
                lat = lat_buf[slot, :span]
                q_lat = q_ref[row]
                q_rot = qr_ref[row]
                s = lax.dot_general(q_lat, lat, nt, preferred_element_type=jnp.float32)
                s = s + jnp.dot(q_rot, rope_buf[slot, :, :span], preferred_element_type=jnp.float32)
                s = s * scale
                own = lax.dot_general(q_lat, nl_all, nt, preferred_element_type=jnp.float32) + lax.dot_general(q_rot, nr_all, nt, preferred_element_type=jnp.float32)
                own = jnp.sum(jnp.where(own_col == row, own, 0.0), axis=1, keepdims=True) * scale
                pos = lax.broadcasted_iota(jnp.int32, (heads, span), 1)
                s = jnp.where(pos < length, s, -jnp.inf)
                top = jnp.maximum(jnp.max(s, axis=1, keepdims=True), own)
                e = jnp.exp(s - top)
                own_e = jnp.exp(own - top)
                inv = 1.0 / (jnp.sum(e, axis=1, keepdims=True) + own_e)
                prob = (e * inv).astype(jnp.bfloat16)
                own_p = (own_e * inv).astype(jnp.bfloat16).astype(jnp.float32)
                acc = jnp.dot(prob, lat, preferred_element_type=jnp.float32)
                acc = acc + own_p * nl_rows[row].astype(jnp.float32)
                mix[row] = acc.astype(jnp.bfloat16)
        return carry

    lax.fori_loop(0, rows, one_row, 0)
    wuv_copy.wait()

    def head_group(grp, carry):
        base = pl.multiple_of(grp * UV_HEADS, UV_HEADS)
        lhs = mix[:, pl.ds(base, UV_HEADS), :].reshape(rows, UV_HEADS * kv_dim)
        rhs = wuv[:, pl.ds(base, UV_HEADS), :].reshape(kv_dim, UV_HEADS * wuv.shape[2])
        v_dim = wuv.shape[2]
        for h in range(UV_HEADS):
            part = jnp.dot(lhs[:, h * kv_dim : (h + 1) * kv_dim], rhs[:, h * v_dim : (h + 1) * v_dim], preferred_element_type=jnp.float32)
            o_ref[:, pl.ds(pl.multiple_of(grp * UV_HEADS * v_dim, v_dim) + h * v_dim, v_dim)] = part.astype(jnp.bfloat16)
        return carry

    lax.fori_loop(0, heads // UV_HEADS, head_group, 0)


def attention(lens, q_abs, q_rope, new_lat, new_rope, cache_lat, rope_t, w_uv):
    rows, heads, kv_dim = q_abs.shape
    cache_len = cache_lat.shape[1]
    rope_dim = q_rope.shape[2]
    v_dim = w_uv.shape[2]
    vmem = pl.BlockSpec(memory_space=pltpu.VMEM)
    hbm = pl.BlockSpec(memory_space=pl.ANY)
    max_blk = cache_len // ATT_BLK
    return pl.pallas_call(
        attn_kernel,
        out_shape=jax.ShapeDtypeStruct((rows, heads * v_dim), jnp.bfloat16),
        in_specs=[pl.BlockSpec(memory_space=pltpu.SMEM), vmem, vmem, vmem, vmem, vmem, hbm, hbm, hbm],
        out_specs=vmem,
        scratch_shapes=[
            pltpu.VMEM((ATT_BUF, cache_len, kv_dim), jnp.bfloat16),
            pltpu.VMEM((ATT_BUF, rope_dim, cache_len), jnp.bfloat16),
            pltpu.VMEM((rows, heads, kv_dim), jnp.bfloat16),
            pltpu.VMEM((kv_dim, heads, v_dim), jnp.bfloat16),
            pltpu.SemaphoreType.DMA((ATT_BUF, max_blk)),
            pltpu.SemaphoreType.DMA((ATT_BUF,)),
            pltpu.SemaphoreType.DMA,
        ],
        compiler_params=pltpu.CompilerParams(vmem_limit_bytes=40 * 2**20),
        cost_estimate=pl.CostEstimate(flops=10**10, bytes_accessed=40 * 10**6, transcendentals=0),
        name="attention",
    )(lens, q_abs, q_rope, new_lat, new_rope, new_lat[:, None, :], cache_lat, rope_t, w_uv)


MESH = pl.DeviceIdType.MESH
RING = 14
TILE_K = 2048
TILE_N = 512
SEND_N = 256


def mlp_kernel(n_dev, o_ref, x_ref, gain_ref, wo_hbm, wg_hbm, wu_hbm, wd_hbm, out_ref,
               ring, o_all, x_all, h_all, m_all, u_own, u_peer, wd_peer, acc, part, own_part, near, relay, far, fin,
               ring_sem, pair_sem, gat_send, gat_recv, u_sem, rs_send, rs_recv):
    rows, d_model = x_ref.shape
    heads_dim = o_ref.shape[1]
    half = d_model // 2
    ff = wg_hbm.shape[1]
    chips = n_dev // 2
    pair = 2 * rows
    total = n_dev * rows
    f32 = jnp.float32
    me = lax.axis_index("g")
    core = me % 2
    chip = me // 2
    peer = chip * 2 + (1 - core)
    right_chip = (chip + 1) % chips
    left_chip = (chip + chips - 1) % chips
    far_chip = (chip + 2) % chips
    right = right_chip * 2 + core
    left = left_chip * 2 + core
    col0 = pl.multiple_of(core * half, half)
    other0 = pl.multiple_of((1 - core) * half, half)

    def remote(src, dst, send, recv, dev):
        return pltpu.make_async_remote_copy(src_ref=src, dst_ref=dst, send_sem=send, recv_sem=recv, device_id={"g": dev}, device_id_type=MESH)

    wo_k = heads_dim // TILE_K
    sub = SEND_N * wo_k
    wo_j = half // TILE_N
    n_wo = wo_j * wo_k
    gu_k = d_model // TILE_K
    gu_n = ff // TILE_N
    n_gu = gu_n * 2 * gu_k
    wd_n = half // TILE_N
    n_all = n_wo + n_gu + wd_n

    def ring_copy(src, slot, depth):
        return pltpu.make_async_copy(src, ring.at[slot, pl.ds(0, depth)], ring_sem.at[slot])

    def issue(t):
        slot = t % RING

        @pl.when(t < n_wo)
        def _():
            j, k = t // wo_k, t % wo_k
            ring_copy(wo_hbm.at[pl.ds(pl.multiple_of(k * TILE_K, TILE_K), TILE_K), pl.ds(pl.multiple_of(col0 + j * TILE_N, TILE_N), TILE_N)], slot, TILE_K).start()

        for mat, w_hbm in ((0, wg_hbm), (1, wu_hbm)):
            q = t - n_wo

            @pl.when((q >= 0) & (q < n_gu) & ((q // gu_k) % 2 == mat))
            def _():
                n, k = q // (2 * gu_k), q % gu_k
                ring_copy(w_hbm.at[pl.ds(pl.multiple_of(k * TILE_K, TILE_K), TILE_K), pl.ds(pl.multiple_of(n * TILE_N, TILE_N), TILE_N)], slot, TILE_K).start()

        @pl.when((t >= n_wo + n_gu) & (t < n_all))
        def _():
            n = t - n_wo - n_gu
            ring_copy(wd_hbm.at[:, pl.ds(pl.multiple_of(col0 + n * TILE_N, TILE_N), TILE_N)], slot, ff).start()

    def arrive(t, depth):
        slot = t % RING
        ring_copy(wo_hbm.at[pl.ds(0, depth), pl.ds(0, TILE_N)], slot, depth).wait()
        return slot

    for t in range(RING):
        issue(jnp.int32(t))

    barrier = pltpu.get_barrier_semaphore()
    for dev in (peer, left, right):
        pl.semaphore_signal(barrier, inc=1, device_id={"g": dev}, device_id_type=MESH)
    pl.semaphore_wait(barrier, 3)

    my_rows = pl.ds(pl.multiple_of(core * rows, rows), rows)
    peer_rows = pl.ds(pl.multiple_of((1 - core) * rows, rows), rows)
    o_copy = remote(o_ref, o_all.at[my_rows], pair_sem.at[0], pair_sem.at[1], peer)
    x_copy = remote(x_ref.at[:, pl.ds(other0, half)], x_all.at[my_rows], pair_sem.at[2], pair_sem.at[3], peer)
    wd_copy = remote(wd_hbm.at[:, pl.ds(other0, half)], wd_peer, pair_sem.at[4], pair_sem.at[5], peer)
    o_copy.start()
    x_copy.start()
    wd_copy.start()
    o_all[my_rows, :] = o_ref[...]
    x_all[my_rows, :] = x_ref[:, pl.ds(col0, half)]
    o_copy.wait()
    x_copy.wait()

    def rows_of(c, lo, num):
        return pl.ds(pl.multiple_of(c * pair + lo, rows), num)

    def chunk_cols(s):
        return pl.ds(pl.multiple_of(col0 + s * SEND_N, SEND_N), SEND_N)

    def near_copy(s, to_right):
        region = h_all.at[rows_of(chip, 0, pair), chunk_cols(s)]
        side = 0 if to_right else 1
        return remote(region, region, gat_send.at[side, s], gat_recv.at[side, s], right if to_right else left)

    def pass_copy(s, to_right):
        src_chip = left_chip if to_right else right_chip
        region = h_all.at[rows_of(src_chip, 0 if to_right else rows, rows), chunk_cols(s)]
        side = 2 if to_right else 3
        return remote(region, region, gat_send.at[side, s], gat_recv.at[side, s], right if to_right else left)

    def peer_copy(s):
        region = h_all.at[:, chunk_cols(s)]
        return remote(region, region, gat_send.at[4, s], gat_recv.at[4, s], peer)

    n_send = half // SEND_N
    per_step = TILE_N // SEND_N

    def gather_step(s):
        for back, act in ((0, 0), (3, 1), (6, 2)):
            c = s - back

            @pl.when((c >= 0) & (c < n_send))
            def _():
                if act == 0:
                    near_copy(c, True).start()
                    near_copy(c, False).start()
                elif act == 1:
                    near_copy(c, True).wait_recv()
                    near_copy(c, False).wait_recv()
                    pass_copy(c, True).start()
                    pass_copy(c, False).start()
                else:
                    pass_copy(c, True).wait_recv()
                    pass_copy(c, False).wait_recv()
                    peer_copy(c).start()

    def wo_step(j, carry):
        for k in range(wo_k):
            if k % (wo_k // per_step) == 0:
                gather_step(per_step * (j - 1) + k // (wo_k // per_step))
            slot = arrive(j * wo_k + k, TILE_K)
            prod = jnp.dot(o_all[:, k * TILE_K : (k + 1) * TILE_K], ring[slot], preferred_element_type=f32)
            if k == 0:
                acc[:pair] = prod
            elif k < wo_k - 1:
                acc[:pair] += prod
            else:
                xs = x_all[:, pl.ds(pl.multiple_of(j * TILE_N, TILE_N), TILE_N)].astype(f32)
                h_all[rows_of(chip, 0, pair), pl.ds(pl.multiple_of(col0 + j * TILE_N, TILE_N), TILE_N)] = (xs + (acc[:pair] + prod)).astype(jnp.bfloat16)
            issue(j * wo_k + k + RING)
        return carry

    lax.fori_loop(0, wo_j, wo_step, 0)

    def drain(s, carry):
        gather_step(s)
        return carry

    lax.fori_loop(per_step * (wo_j - 1), n_send + 6, drain, 0)

    def settle(s, carry):
        peer_copy(s).wait()
        for to_right in (True, False):
            near_copy(s, to_right).wait_send()
            pass_copy(s, to_right).wait_send()
        return carry

    lax.fori_loop(0, n_send, settle, 0)

    def norm_rows(b, carry):
        block = pl.ds(pl.multiple_of(b * 16, 16), 16)
        lanes = jnp.zeros((16, 128), f32)
        for c in range(0, d_model, 512):
            v = h_all[block, c : c + 512].astype(f32)
            sq = v * v
            lanes = lanes + ((sq[:, :128] + sq[:, 128:256]) + (sq[:, 256:384] + sq[:, 384:]))
        inv = lax.rsqrt(jnp.sum(lanes, axis=1, keepdims=True) / d_model + 1e-6)
        for c in range(0, d_model, 512):
            v = h_all[block, c : c + 512].astype(f32)
            m_all[block, c : c + 512] = (v * inv * gain_ref[:, c : c + 512].astype(f32)).astype(jnp.bfloat16)
        return carry

    lax.fori_loop(0, total // 16, norm_rows, 0)

    def u_copy(n):
        span = pl.ds(pl.multiple_of(n * TILE_N, TILE_N), TILE_N)
        return remote(u_own.at[:, span], u_peer.at[:, span], u_sem.at[0, n], u_sem.at[1, n], peer)

    def gu_step(n, carry):
        for mat in range(2):
            for k in range(gu_k):
                t = n_wo + n * 2 * gu_k + mat * gu_k + k
                slot = arrive(t, TILE_K)
                prod = jnp.dot(m_all[:, k * TILE_K : (k + 1) * TILE_K], ring[slot], preferred_element_type=f32)
                if k == 0:
                    acc[pl.ds(mat * total, total)] = prod
                else:
                    acc[pl.ds(mat * total, total)] += prod
                issue(t + RING)
        span = pl.ds(pl.multiple_of(n * TILE_N, TILE_N), TILE_N)
        for b in range(0, total, 64):
            g = acc[b : b + 64]
            u_own[b : b + 64, span] = (jax.nn.silu(g) * acc[total + b : total + b + 64]).astype(jnp.bfloat16)
        u_copy(n).start()
        return carry

    lax.fori_loop(0, gu_n, gu_step, 0)
    wd_copy.wait()
    for n in range(gu_n):
        u_copy(n).wait()

    def span_of(n):
        return pl.ds(pl.multiple_of(n * TILE_N, TILE_N), TILE_N)

    def rs_near(n, to_right):
        side = 0 if to_right else 1
        c = right_chip if to_right else left_chip
        return remote(part.at[rows_of(c, 0, pair), span_of(n)], near.at[side, :, span_of(n)], rs_send.at[side, n], rs_recv.at[side, n], right if to_right else left)

    def rs_far(n, to_right):
        side = 0 if to_right else 1
        return remote(part.at[rows_of(far_chip, side * rows, rows), span_of(n)], relay.at[side, :, span_of(n)], rs_send.at[2 + side, n], rs_recv.at[2 + side, n], right if to_right else left)

    def rs_pass(n, to_right):
        side = 0 if to_right else 1
        return remote(relay.at[side, :, span_of(n)], far.at[side, :, span_of(n)], rs_send.at[4 + side, n], rs_recv.at[4 + side, n], right if to_right else left)

    def out_cols(n):
        return pl.ds(pl.multiple_of(col0 + n * TILE_N, TILE_N), TILE_N)

    def rs_out(n):
        return remote(fin.at[:, span_of(n)], out_ref.at[:, out_cols(n)], rs_send.at[6, n], rs_recv.at[6, n], peer)

    def down_step(n, carry):
        t = n_wo + n_gu + n
        slot = arrive(t, ff)
        acc[:total] = jnp.dot(u_own[...], ring[slot, :ff], preferred_element_type=f32)
        acc[:total] += jnp.dot(u_peer[...], wd_peer[:, span_of(n)], preferred_element_type=f32)
        part[:, span_of(n)] = acc[:total].astype(jnp.bfloat16)
        own_part[:, span_of(n)] = acc[rows_of(chip, 0, pair), :]
        for to_right in (True, False):
            rs_far(n, to_right).start()
        for to_right in (True, False):
            rs_near(n, to_right).start()
        return carry

    lax.fori_loop(0, wd_n, down_step, 0)

    def final_step(s, carry):
        @pl.when(s < wd_n)
        def _():
            for to_right in (True, False):
                rs_far(s, to_right).wait_recv()
                rs_pass(s, to_right).start()

        @pl.when(s >= 1)
        def _():
            n = s - 1
            for to_right in (True, False):
                rs_near(n, to_right).wait_recv()
                rs_pass(n, to_right).wait_recv()
            span = span_of(n)

            def rows_sum(lo_static, lo):
                blk = pl.ds(pl.multiple_of(lo, rows), rows)
                mlp = own_part[blk, span] + near[0, blk, span].astype(f32) + near[1, blk, span].astype(f32) + far[lo_static, :, span].astype(f32)
                return (h_all[rows_of(chip, lo, rows), out_cols(n)].astype(f32) + mlp).astype(jnp.bfloat16)

            low = rows_sum(0, 0)
            high = rows_sum(1, rows)
            mine = jnp.where(core == 0, low, high)
            out_ref[:, out_cols(n)] = mine
            fin[:, span] = jnp.where(core == 0, high, low)
            rs_out(n).start()

        return carry

    lax.fori_loop(0, wd_n + 1, final_step, 0)

    def finish(n, carry):
        rs_out(n).wait()
        for to_right in (True, False):
            rs_near(n, to_right).wait_send()
            rs_far(n, to_right).wait_send()
            rs_pass(n, to_right).wait_send()
        return carry

    lax.fori_loop(0, wd_n, finish, 0)


def out_proj_mlp(n_dev, o, x, gain, w_o, w_gate, w_up, w_down):
    rows, d_model = x.shape
    half = d_model // 2
    ff = w_gate.shape[1]
    pair, total = 2 * rows, n_dev * rows
    bf16, f32 = jnp.bfloat16, jnp.float32
    vmem = pl.BlockSpec(memory_space=pltpu.VMEM)
    hbm = pl.BlockSpec(memory_space=pl.ANY)
    n_send, wd_n = half // SEND_N, half // TILE_N
    dma = pltpu.SemaphoreType.DMA
    return pl.pallas_call(
        functools.partial(mlp_kernel, n_dev),
        out_shape=jax.ShapeDtypeStruct((rows, d_model), bf16),
        in_specs=[vmem, vmem, vmem, hbm, hbm, hbm, hbm],
        out_specs=vmem,
        scratch_shapes=[
            pltpu.VMEM((RING, TILE_K, TILE_N), bf16),
            pltpu.VMEM((pair, o.shape[1]), bf16),
            pltpu.VMEM((pair, half), bf16),
            pltpu.VMEM((total, d_model), bf16),
            pltpu.VMEM((total, d_model), bf16),
            pltpu.VMEM((total, ff), bf16),
            pltpu.VMEM((total, ff), bf16),
            pltpu.VMEM((ff, half), bf16),
            pltpu.VMEM((2 * total, TILE_N), f32),
            pltpu.VMEM((total, half), bf16),
            pltpu.VMEM((pair, half), f32),
            pltpu.VMEM((2, pair, half), bf16),
            pltpu.VMEM((2, rows, half), bf16),
            pltpu.VMEM((2, rows, half), bf16),
            pltpu.VMEM((rows, half), bf16),
            dma((RING,)),
            dma((6,)),
            dma((5, n_send)),
            dma((5, n_send)),
            dma((2, ff // TILE_N)),
            dma((7, wd_n)),
            dma((7, wd_n)),
        ],
        compiler_params=pltpu.CompilerParams(vmem_limit_bytes=67043328, collective_id=1, has_side_effects=True),
        cost_estimate=pl.CostEstimate(flops=2 * 10**10, bytes_accessed=116 * 10**6, transcendentals=0),
        name="out_proj_mlp",
    )(o, x, gain, w_o, w_gate, w_up, w_down)


def attention_rows(hidden, cache_lat, cache_rope, seq_lens, gain_attn, w_dq, gain_q, w_uq, w_qr, w_dkv, gain_kv, w_uk, w_uv, w_o):
    kv_dim = w_uk.shape[0]
    normed = rms_norm(hidden.astype(jnp.float32), gain_attn).astype(jnp.bfloat16)
    q_in = rms_norm(jnp.dot(normed, w_dq, preferred_element_type=jnp.float32), gain_q).astype(jnp.bfloat16)
    q_nope = jnp.einsum("bq,qhn->bhn", q_in, w_uq, preferred_element_type=jnp.float32).astype(jnp.bfloat16)
    q_rope = apply_rope(jnp.einsum("bq,qhr->bhr", q_in, w_qr, preferred_element_type=jnp.float32), seq_lens[:, None]).astype(jnp.bfloat16)
    kv_raw = jnp.dot(normed, w_dkv, preferred_element_type=jnp.float32)
    new_lat = rms_norm(kv_raw[:, :kv_dim], gain_kv).astype(jnp.bfloat16)
    new_rope = apply_rope(kv_raw[:, kv_dim:], seq_lens).astype(jnp.bfloat16)
    q_abs = jnp.einsum("bhn,chn->bhc", q_nope, w_uk, preferred_element_type=jnp.float32).astype(jnp.bfloat16)
    out_heads = attention(seq_lens, q_abs, q_rope, new_lat, new_rope, cache_lat, jnp.swapaxes(cache_rope, 1, 2), w_uv)
    return out_heads, new_lat, new_rope


def solution(mesh):
    row_spec = P(("rep", "g"))
    full_spec = P()
    in_specs = (row_spec, row_spec, row_spec, row_spec, full_spec, full_spec, full_spec, full_spec, full_spec, full_spec, full_spec, full_spec, full_spec, full_spec, full_spec, P(None, "g"), P(None, "g"), P("g", None))

    def local_step(hidden, cache_lat, cache_rope, seq_lens, gain_attn, w_dq, gain_q, w_uq, w_qr, w_dkv, gain_kv, w_uk, w_uv, w_o, gain_mlp, w_gate, w_up, w_down):
        out_heads, new_lat, new_rope = attention_rows(hidden, cache_lat, cache_rope, seq_lens, gain_attn, w_dq, gain_q, w_uq, w_qr, w_dkv, gain_kv, w_uk, w_uv, w_o)
        out_hidden = out_proj_mlp(mesh.shape["g"], out_heads, hidden, gain_mlp[None, :], w_o, w_gate, w_up, w_down)
        return out_hidden, new_lat, new_rope

    return jax.shard_map(local_step, mesh=mesh, in_specs=in_specs, out_specs=(row_spec, row_spec, row_spec), check_vma=False)
```

profile of v0, /device:TPU:113, one launch (start us, length us, event | category | flops | bytes accessed | tf_op | source)
XLA Modules:
  0.0 175.2 jit_solution(6830841845521348908)
XLA Ops:
  0.6 0.7 convert_element_type.49
  1.3 0.0 slice-start
  1.3 1.3 fusion.8
  2.7 0.0 copy-start.7
  2.7 0.0 slice-start.1
  2.7 0.0 slice-start.2
  2.7 8.6 %multiply_reduce_fusion = (f32[32]{0:T(128)S(1)}, f32[32,1536]{1,0:T(8,128)S(1)}) fusion(bf16[6144,1536]{1,0:T(8,128)(2,1)} %param.23, bf16[32,6144]{1,0:T(8,128)(2,1)} %x_ref.1, f32[6144]{0:T(1024)S(1)} %convert_element_type.49, f32[32]{0:T(128)S(1)} %add_rsqrt_fusion.2), kind=kOutput, calls=%fused_computation.16 | convolution fusion | flops 604864512 | bytes 19489024 | tf_op jit(solution)/shard_map/dot_general | solution.py:489
  11.3 0.0 copy-start.5
  11.3 0.0 copy-done.7
  11.3 0.0 slice-done
  11.3 0.0 slice-done.1
  11.3 0.5 slice-done.2
  11.8 0.0 copy-start.4
  11.8 0.0 copy-start.8
  11.8 5.8 %fusion.18 = f32[32,64,64]{2,0,1:T(8,128)S(1)} fusion(bf16[1536,64,64]{0,2,1:T(8,128)(2,1)S(1)} %bitcast.17, f32[32,1536]{1,0:T(8,128)S(1)} %get-tuple-element.12, f32[1536]{0:T(1024)S(1)} %convert_element_type.51, f32[32]{0:T(128)S(1)} %add_rsqrt_fusion.1), kind=kOutput, calls=%fused_computation.31 | convolution fusion | flops 402800640 | bytes 13310080 | tf_op jit(solution)/shard_map/bq,qhr->bhr/dot_general | solution.py:491
  17.6 0.4 fusion.22
  18.0 0.0 copy-done.5
  18.0 5.1 %fusion.13 = f32[32,576]{1,0:T(8,128)S(1)} fusion(bf16[6144,576]{0,1:T(8,128)(2,1)} %param.27, bf16[32,6144]{1,0:T(8,128)(2,1)S(1)} %copy-done.5, f32[6144]{0:T(1024)S(1)} %convert_element_type.49, f32[32]{0:T(128)S(1)} %add_rsqrt_fusion.2), kind=kOutput, calls=%fused_computation.17 | convolution fusion | flops 227278848 | bytes 7569536 | tf_op jit(solution)/shard_map/dot_general | solution.py:492
  23.1 0.0 copy-done.4
  23.2 0.1 subtract_convert_fusion.1
  23.3 1.4 subtract_convert_fusion
  24.7 0.3 pad_maximum_fusion.qr_ref
  25.0 0.1 pad_maximum_fusion.1.nr_ref
  25.1 0.0 copy-start.3
  25.1 0.1 multiply_reduce_fusion.1
  25.2 0.0 copy-done.8
  25.2 0.1 multiply_convert_fusion.1.nl_ref
  25.3 0.0 copy-start.2
  25.3 0.1 fusion.26
  25.4 0.1 copy.29.nl_rows
  25.4 29.2 %fusion.2 = bf16[64,32,512]{2,1,0:T(8,128)(2,1)S(1)} fusion(bf16[512,64,128]{2,1,0:T(8,128)(2,1)} %param.29, bf16[1536,64,128]{2,1,0:T(8,128)(2,1)} %param.25, f32[32,1536]{1,0:T(8,128)S(1)} %get-tuple-element.12, f32[1536]{0:T(1024)S(1)} %convert_element_type.51, f32[32]{0:T(128)S(1)} %add_rsqrt_fusion.1), kind=kOutput, calls=%fused_computation.2 | convolution fusion | flops 1074151424 | bytes 35854464 | tf_op jit(solution)/shard_map/bhn,chn->bhc/dot_general | solution.py:495
  54.6 1.2 copy.48
  55.8 0.0 copy-done.3
  55.8 0.0 copy-done.2
  55.8 0.0 copy-start
  55.8 2.2 %copy-done = bf16[32,1024,64]{1,2,0:T(8,128)(2,1)S(1)} copy-done((bf16[32,1024,64]{1,2,0:T(8,128)(2,1)S(1)}, bf16[32,1024,64]{1,2,0:T(8,128)(2,1)}, u32[]{:S(2)}) %copy-start) | copy-done | bytes 4194328
  58.0 0.0 copy-start.6
  58.0 40.8 %attention.1.o_ref = bf16[32,8192]{1,0:T(8,128)(2,1)S(1)} custom-call(s32[32]{0:T(128)S(1)} %copy-done.4, bf16[32,64,512]{2,1,0:T(8,128)(2,1)S(1)} %bitcast.14, bf16[32,64,64]{2,1,0:T(8,128)(2,1)S(1)} %pad_maximum_fusion.qr_ref, bf16[32,512]{1,0:T(8,128)(2,1)S(1)} %multiply_convert_fusion.1.nl_ref, bf16[32,64]{1,0:T(8,128)(2,1)S(1)} %pad_maximum_fusion.1.nr_ref, ...), custom_call_target="tpu_custom_call" | custom-call | flops 10000000000 | bytes 40000000 | tf_op jit(solution)/shard_map/attention/pallas_call | solution.py:131
  98.8 0.0 copy-start.1
  98.8 0.8 copy-done.1
  99.6 0.0 copy-done.6
  99.6 0.6 broadcast_in_dim.5.gain_ref
  100.2 73.2 %out_proj_mlp.1 = bf16[32,6144]{1,0:T(8,128)(2,1)} custom-call(bf16[32,8192]{1,0:T(8,128)(2,1)} %copy-done.1, bf16[32,6144]{1,0:T(8,128)(2,1)} %x_ref.1, bf16[1,6144]{1,0:T(2,128)(2,1)} %broadcast_in_dim.5.gain_ref, bf16[8192,6144]{1,0:T(8,128)(2,1)} %wo_hbm.1, bf16[6144,1536]{1,0:T(8,128)(2,1)} %wg_hbm.1, bf16[6144,1536]{1,0:T(8,128)(2,1)} %wu_hbm.1, ...), custom_call_target="tpu_custom_call" | custom-call | flops 20000000000 | bytes 116000000 | tf_op jit(solution)/shard_map/out_proj_mlp/pallas_call | solution.py:451
  173.4 1.8 %copy.50 = bf16[32,6144]{1,0:T(8,128)(2,1)} copy(bf16[32,6144]{1,0:T(8,128)(2,1)} %out_proj_mlp.1) | data formatting | bytes 786432
  (8 shorter events, 0.1 us)
Async XLA Ops:
  1.3 10.0 %slice-start = ((s8[12582912]{0:T(1024)(128)(4,1)}), s8[4194304]{0:T(1024)(128)(4,1)S(1)}, s32[]{:S(2)}) async-start(s8[12582912]{0:T(1024)(128)(4,1)} %bitcast.16), calls=%async_computation | async-start | bytes 8388608
  2.7 8.6 %copy-start.7 = (bf16[1536]{0:T(1024)(128)(2,1)S(1)}, bf16[1536]{0:T(1024)(128)(2,1)}, u32[]{:S(2)}) copy-start(bf16[1536]{0:T(1024)(128)(2,1)} %param.24) | copy-start | bytes 9220
  2.7 8.6 %slice-start.1 = ((s8[12582912]{0:T(1024)(128)(4,1)}), s8[4194304]{0:T(1024)(128)(4,1)S(1)}, s32[]{:S(2)}) async-start(s8[12582912]{0:T(1024)(128)(4,1)} %bitcast.16), calls=%async_computation.1 | async-start | bytes 8388608
  2.7 9.1 %slice-start.2 = ((s8[12582912]{0:T(1024)(128)(4,1)}), s8[4194304]{0:T(1024)(128)(4,1)S(1)}, s32[]{:S(2)}) async-start(s8[12582912]{0:T(1024)(128)(4,1)} %bitcast.16), calls=%async_computation.2 | async-start | bytes 8388608
  11.3 6.7 %copy-start.5 = (bf16[32,6144]{1,0:T(8,128)(2,1)S(1)}, bf16[32,6144]{1,0:T(8,128)(2,1)}, u32[]{:S(2)}) copy-start(bf16[32,6144]{1,0:T(8,128)(2,1)} %x_ref.1) | copy-start | bytes 1179652
  11.8 11.3 %copy-start.4 = (s32[32]{0:T(128)S(1)}, s32[32]{0:T(128)}, u32[]{:S(2)}) copy-start(s32[32]{0:T(128)} %lens_ref.1) | copy-start | bytes 388
  11.8 13.4 %copy-start.8 = (bf16[512]{0:T(512)(128)(2,1)S(1)}, bf16[512]{0:T(512)(128)(2,1)}, u32[]{:S(2)}) copy-start(bf16[512]{0:T(512)(128)(2,1)} %param.28) | copy-start | bytes 3076
  25.1 30.7 %copy-start.3 = (bf16[32,64]{1,0:T(8,128)(2,1)}, bf16[32,64]{1,0:T(8,128)(2,1)S(1)}, u32[]{:S(2)}) copy-start(bf16[32,64]{1,0:T(8,128)(2,1)S(1)} %pad_maximum_fusion.1.nr_ref) | copy-start | bytes 12292
  25.3 30.5 %copy-start.2 = (bf16[32,512]{1,0:T(8,128)(2,1)}, bf16[32,512]{1,0:T(8,128)(2,1)S(1)}, u32[]{:S(2)}) copy-start(bf16[32,512]{1,0:T(8,128)(2,1)S(1)} %multiply_convert_fusion.1.nl_ref) | copy-start | bytes 98308
  55.8 2.2 %copy-start = (bf16[32,1024,64]{1,2,0:T(8,128)(2,1)S(1)}, bf16[32,1024,64]{1,2,0:T(8,128)(2,1)}, u32[]{:S(2)}) copy-start(bf16[32,1024,64]{1,2,0:T(8,128)(2,1)} %param.20) | copy-start | bytes 12582916
  58.0 41.6 %copy-start.6 = (bf16[6144]{0:T(1024)(128)(2,1)S(1)}, bf16[6144]{0:T(1024)(128)(2,1)}, u32[]{:S(2)}) copy-start(bf16[6144]{0:T(1024)(128)(2,1)} %param.32) | copy-start | bytes 36868
  98.8 0.8 copy-start.1
where the time goes:
time: 175 us
  Pallas kernels  114 us (65%)
  matrix products  48.6 us (28%)
  local copies, waits for them, and re-layouts  7.5 us (4%)
  other arithmetic  4.23 us (2%)
    pallas_call x1, Pallas kernels, out_proj_mlp(): pl.pallas_call(functools.partial(mlp_kernel, n_dev), out_shape=jax.ShapeD...  73.2 us
    pallas_call x1, Pallas kernels, attention(): pl.pallas_call(attn_kernel, out_shape=jax.ShapeDtypeStruct((rows, heads *...  40.8 us
    dot_general x1, matrix products, attention_rows(): jnp.einsum('bhn,chn->bhc', q_nope, w_uk, preferred_element_type=jnp.float32)  29.2 us
    dot_general x1, matrix products, attention_rows(): jnp.dot(normed, w_dq, preferred_element_type=jnp.float32)  8.55 us
    dot_general x1, matrix products, attention_rows(): jnp.einsum('bq,qhr->bhr', q_in, w_qr, preferred_element_type=jnp.float32)  5.78 us
    unnamed x25, local copies, waits for them, and re-layouts  5.28 us
    dot_general x1, matrix products, attention_rows(): kv_raw = jnp.dot(normed, w_dkv, preferred_element_type=jnp.float32)  5.13 us

commit v1 on v0

v1 whole, which is shorter than its diff:
```python
import functools

import jax
import jax.numpy as jnp
import numpy as np
from jax import lax
from jax.experimental import pallas as pl
from jax.experimental.pallas import tpu as pltpu
from jax.sharding import PartitionSpec as P

MESH = pl.DeviceIdType.MESH
HEAD_GRP = 16
DQ_K = 1024


def proj_kernel(n_dev, lens_ref, x_ref, freq_ref, ga_ref, gq_ref, gkv_ref, wdq_hbm, wdkv_hbm, wuq_hbm, wqr_hbm, wuk_hbm,
                q_out, q2_out, nl_out, nr_out,
                wdq, wdkv, wuq, wqr, wuk, a_all, t_all, c_all, ang, kv_buf, kv_send, qh, qx, rh, rx,
                w_sem, x_sem, q_sem):
    rows, d_model = x_ref.shape
    f32, bf16 = jnp.float32, jnp.bfloat16
    nt = (((1,), (1,)), ((), ()))
    pair = 2 * rows
    q_half = wdq.shape[1]
    q_dim = 2 * q_half
    kv_dim = gkv_ref.shape[0] * 128
    kv_cols = wdkv.shape[0]
    kv_lo = kv_dim // 2
    n_grp = wuq.shape[0]
    my_heads = n_grp * HEAD_GRP
    n_dim = wuq.shape[3]
    me = lax.axis_index("g")
    core = me % 2
    peer = me + 1 - 2 * core
    my_rows = pl.ds(pl.multiple_of(core * rows, rows), rows)
    peer_rows = pl.ds(pl.multiple_of((1 - core) * rows, rows), rows)
    n_dq = d_model // DQ_K
    loads = []
    for k in range(n_dq):
        loads.append(pltpu.make_async_copy(wdq_hbm.at[pl.ds(k * DQ_K, DQ_K), pl.ds(pl.multiple_of(core * q_half, q_half), q_half)], wdq.at[pl.ds(k * DQ_K, DQ_K)], w_sem.at[k]))
    dkv_load = pltpu.make_async_copy(wdkv_hbm.at[pl.ds(pl.multiple_of(core * kv_lo, kv_lo), kv_cols)], wdkv, w_sem.at[n_dq])
    loads.append(dkv_load)
    uq_loads, uk_loads = [], []
    for g in range(n_grp):
        heads = pl.ds(pl.multiple_of(core * my_heads + g * HEAD_GRP, HEAD_GRP), HEAD_GRP)
        uq_loads.append(pltpu.make_async_copy(wuq_hbm.at[:, heads], wuq.at[g], w_sem.at[n_dq + 1 + g]))
        uk_loads.append(pltpu.make_async_copy(wuk_hbm.at[:, heads], wuk.at[g], w_sem.at[n_dq + 1 + n_grp + g]))
        loads += [uq_loads[g], uk_loads[g]]
    qr_rows = wqr.shape[0]
    qr_load = pltpu.make_async_copy(wqr_hbm.at[pl.ds(pl.multiple_of(core * qr_rows, qr_rows), qr_rows)], wqr, w_sem.at[n_dq + 1 + 2 * n_grp])
    loads.append(qr_load)
    for cp in loads:
        cp.start()

    def remote(src, dst, i):
        return pltpu.make_async_remote_copy(src_ref=src, dst_ref=dst, send_sem=x_sem.at[0, i], recv_sem=x_sem.at[1, i], device_id={"g": peer}, device_id_type=MESH)

    row_id = lax.broadcasted_iota(jnp.int32, (rows, 128), 0)
    pos = jnp.zeros((rows, 128), jnp.int32)
    for r in range(rows):
        pos = jnp.where(row_id == r, lens_ref[r], pos)
    ang[my_rows, :] = pos.astype(f32) * freq_ref[...]
    lanes = jnp.zeros((rows, 128), f32)
    for c in range(0, d_model, 512):
        v = x_ref[:, c : c + 512].astype(f32)
        sq = v * v
        lanes = lanes + ((sq[:, :128] + sq[:, 128:256]) + (sq[:, 256:384] + sq[:, 384:]))
    inv = lax.rsqrt(jnp.sum(lanes, axis=1, keepdims=True) / d_model + 1e-6)
    ga_rows = ga_ref[...].astype(f32)
    for c in range(0, d_model, 128):
        v = x_ref[:, c : c + 128].astype(f32)
        a_all[my_rows, c : c + 128] = (v * inv * ga_rows[c // 128 : c // 128 + 1]).astype(bf16)
    barrier = pltpu.get_barrier_semaphore()
    pl.semaphore_signal(barrier, inc=1, device_id={"g": peer}, device_id_type=MESH)
    pl.semaphore_wait(barrier, 1)
    a_copy = remote(a_all.at[my_rows], a_all.at[my_rows], 0)
    ang_copy = remote(ang.at[my_rows], ang.at[my_rows], 1)
    a_copy.start()
    ang_copy.start()
    a_copy.wait()
    ang_copy.wait()

    t = jnp.zeros((pair, q_half), f32)
    for k in range(n_dq):
        loads[k].wait()
        t = t + jnp.dot(a_all[:, k * DQ_K : (k + 1) * DQ_K], wdq[k * DQ_K : (k + 1) * DQ_K], preferred_element_type=f32)
    t_all[core] = t
    t_copy = remote(t_all.at[core], t_all.at[core], 2)
    t_copy.start()

    dkv_load.wait()
    kv_send[:, :kv_cols] = lax.dot_general(a_all[...], wdkv[...], nt, preferred_element_type=f32)
    kv_send[:, kv_cols:] = jnp.zeros((pair, kv_send.shape[1] - kv_cols), f32)
    kv_copy = remote(kv_send.at[peer_rows], kv_buf.at[core], 3)
    kv_copy.start()
    kv_buf[core] = kv_send[my_rows, :]

    lane = lax.broadcasted_iota(jnp.int32, (1, 128), 1)
    low_half = lane % 64 < 32
    cos_all = jnp.cos(ang[...])
    sin_all = jnp.where(low_half, -jnp.sin(ang[...]), jnp.sin(ang[...]))

    def rope(v, cos_part, sin_part):
        swapped = jnp.where(low_half, pltpu.roll(v, 96, 1), pltpu.roll(v, 32, 1))
        return (v * cos_part + swapped * sin_part).astype(bf16)

    t_copy.wait()
    t0, t1 = t_all[0], t_all[1]
    inv = lax.rsqrt((jnp.sum(t0 * t0, axis=1, keepdims=True) + jnp.sum(t1 * t1, axis=1, keepdims=True)) / q_dim + 1e-6)
    gq_rows = gq_ref[...].astype(f32)
    for c in range(0, q_dim, 128):
        piece = t0[:, c : c + 128] if c < q_half else t1[:, c - q_half : c - q_half + 128]
        c_all[:, c : c + 128] = (piece * inv * gq_rows[c // 128 : c // 128 + 1]).astype(bf16)

    half_grp = HEAD_GRP // 2
    q_copies = []
    for g in range(n_grp):
        uq_loads[g].wait()
        w = wuq[g].reshape(q_dim, HEAD_GRP * n_dim)
        q_nope = jnp.dot(c_all[...], w, preferred_element_type=f32).astype(bf16)
        uk_loads[g].wait()
        w = wuk[g].reshape(kv_dim, HEAD_GRP * n_dim)
        for hh in range(HEAD_GRP):
            at = (hh % 2) * (my_heads // 2) + g * half_grp + hh // 2
            span = slice(hh * n_dim, (hh + 1) * n_dim)
            qh[at] = lax.dot_general(q_nope[:, span], w[:, span], nt, preferred_element_type=f32).astype(bf16)
        for odd in range(2):
            at = pl.ds(odd * (my_heads // 2) + g * half_grp, half_grp)
            i = 2 * g + odd
            cp = pltpu.make_async_remote_copy(src_ref=qh.at[at, peer_rows], dst_ref=qx.at[at], send_sem=q_sem.at[0, i], recv_sem=q_sem.at[1, i], device_id={"g": peer}, device_id_type=MESH)
            cp.start()
            q_copies.append(cp)

    qr_load.wait()
    blk = 512
    for b in range(qr_rows // blk):
        v = lax.dot_general(c_all[...], wqr[b * blk : (b + 1) * blk], nt, preferred_element_type=f32)
        for p in range(blk // 128):
            rh[b * (blk // 128) + p] = rope(v[:, p * 128 : (p + 1) * 128], cos_all, sin_all)
    r_copy = remote(rh.at[:, peer_rows], rx, 4)
    r_copy.start()

    kv_copy.wait()
    k0, k1 = kv_buf[0], kv_buf[1]
    lo, hi = k0[:, :kv_lo], k1[:, :kv_lo]
    inv = lax.rsqrt((jnp.sum(lo * lo, axis=1, keepdims=True) + jnp.sum(hi * hi, axis=1, keepdims=True)) / kv_dim + 1e-6)
    gkv_rows = gkv_ref[...].astype(f32)
    for c in range(0, kv_dim, 128):
        piece = lo[:, c : c + 128] if c < kv_lo else hi[:, c - kv_lo : c - kv_lo + 128]
        nl_out[:, c : c + 128] = (piece * inv * gkv_rows[c // 128 : c // 128 + 1]).astype(bf16)
    ang_mine = ang[my_rows, :]
    nr = rope(k1[:, kv_lo : kv_lo + 128], jnp.cos(ang_mine), jnp.where(low_half, -jnp.sin(ang_mine), jnp.sin(ang_mine)))
    nr_out[...] = nr[:, : nr_out.shape[1]]

    own0 = core * my_heads
    other0 = (1 - core) * my_heads
    for p in range(0, my_heads, 16):
        q_out[:, pl.ds(pl.multiple_of(own0 + p, 16), 16), :] = jnp.swapaxes(qh[p : p + 16, my_rows, :], 0, 1)
    for cp in q_copies:
        cp.wait()
    for p in range(0, my_heads, 16):
        q_out[:, pl.ds(pl.multiple_of(other0 + p, 16), 16), :] = jnp.swapaxes(qx[p : p + 16], 0, 1)
    n_pair = my_heads // 2
    q2_out[:, pl.ds(pl.multiple_of(core * n_pair, n_pair), n_pair), :] = jnp.swapaxes(rh[:, my_rows, :], 0, 1)
    r_copy.wait()
    q2_out[:, pl.ds(pl.multiple_of((1 - core) * n_pair, n_pair), n_pair), :] = jnp.swapaxes(rx[...], 0, 1)


def projections(n_dev, lens, x, gain_attn, w_dq, gain_q, w_uq, w_qr, w_dkv, gain_kv, w_uk):
    rows, d_model = x.shape
    q_dim, n_heads, n_dim = w_uq.shape
    kv_dim = w_uk.shape[0]
    rope_dim = w_qr.shape[2]
    my_heads = n_heads // 2
    n_grp = my_heads // HEAD_GRP
    pair = 2 * rows
    bf16, f32 = jnp.bfloat16, jnp.float32
    half_rope = rope_dim // 2
    kv_cols = kv_dim // 2 + rope_dim
    kv_wide = -(-kv_cols // 128) * 128
    freq = np.tile(np.float32(10000.0) ** (-np.arange(half_rope, dtype=np.float32) / np.float32(half_rope)), 128 // half_rope)[None, :].astype(np.float32)
    vmem = pl.BlockSpec(memory_space=pltpu.VMEM)
    hbm = pl.BlockSpec(memory_space=pl.ANY)
    dma = pltpu.SemaphoreType.DMA
    qr_rows = my_heads * rope_dim
    return pl.pallas_call(
        functools.partial(proj_kernel, n_dev),
        out_shape=(
            jax.ShapeDtypeStruct((rows, n_heads, kv_dim), bf16),
            jax.ShapeDtypeStruct((rows, n_heads // 2, 2 * rope_dim), bf16),
            jax.ShapeDtypeStruct((rows, kv_dim), bf16),
            jax.ShapeDtypeStruct((rows, rope_dim), bf16),
        ),
        in_specs=[pl.BlockSpec(memory_space=pltpu.SMEM), vmem, vmem, vmem, vmem, vmem, hbm, hbm, hbm, hbm, hbm],
        out_specs=(vmem, vmem, vmem, vmem),
        scratch_shapes=[
            pltpu.VMEM((d_model, q_dim // 2), bf16),
            pltpu.VMEM((kv_cols, d_model), bf16),
            pltpu.VMEM((n_grp, q_dim, HEAD_GRP, n_dim), bf16),
            pltpu.VMEM((qr_rows, q_dim), bf16),
            pltpu.VMEM((n_grp, kv_dim, HEAD_GRP, n_dim), bf16),
            pltpu.VMEM((pair, d_model), bf16),
            pltpu.VMEM((2, pair, q_dim // 2), f32),
            pltpu.VMEM((pair, q_dim), bf16),
            pltpu.VMEM((pair, 128), f32),
            pltpu.VMEM((2, rows, kv_wide), f32),
            pltpu.VMEM((pair, kv_wide), f32),
            pltpu.VMEM((my_heads, pair, kv_dim), bf16),
            pltpu.VMEM((my_heads, rows, kv_dim), bf16),
            pltpu.VMEM((my_heads // 2, pair, 128), bf16),
            pltpu.VMEM((my_heads // 2, rows, 128), bf16),
            dma((d_model // DQ_K + 2 + 2 * n_grp,)),
            dma((2, 5)),
            dma((2, 2 * n_grp)),
        ],
        compiler_params=pltpu.CompilerParams(vmem_limit_bytes=67043328, collective_id=0, has_side_effects=True),
        cost_estimate=pl.CostEstimate(flops=5 * 10**9, bytes_accessed=40 * 10**6, transcendentals=0),
        name="projections",
    )(lens, x, freq, gain_attn.reshape(-1, 128), gain_q.reshape(-1, 128), gain_kv.reshape(-1, 128), w_dq, w_dkv.T, w_uq, jnp.transpose(w_qr, (1, 2, 0)).reshape(-1, q_dim), w_uk)


ATT_BLK = 256
ATT_BUF = 8
UV_HEADS = 16


def attn_kernel(lens_ref, q_hbm, q2_hbm, nl_hbm, nr_hbm, lat_hbm, rope_hbm, wuv_hbm, o_ref, nl_out, nr_out,
                lat_buf, rope_buf, mix, wuv, q_all, q2_all, nl_rows, order, fill, lat_sem, rope_sem, in_sem):
    rows, heads, kv_dim = q_all.shape
    cache_len = lat_hbm.shape[1]
    r_dim = nr_out.shape[1]
    scale = (wuv.shape[2] + r_dim) ** -0.5
    max_blk = cache_len // ATT_BLK
    n_pair = heads // 4
    f32 = jnp.float32

    def blocks(row):
        return (lens_ref[row] + ATT_BLK - 1) // ATT_BLK

    start = jnp.int32(0)
    for num in range(1, max_blk + 1):
        fill[num] = start
        for row in range(rows):
            start = start + (blocks(row) == num).astype(jnp.int32)

    def place(row, carry):
        num = blocks(row)
        at = fill[num]
        order[at] = row
        fill[num] = at + 1
        return carry

    lax.fori_loop(0, rows, place, 0)

    def lat_copy(row, blk, slot):
        span = pl.ds(blk * ATT_BLK, ATT_BLK)
        return pltpu.make_async_copy(lat_hbm.at[row, span], lat_buf.at[slot, span], lat_sem.at[slot, blk])

    def rope_copy(row, slot):
        return pltpu.make_async_copy(rope_hbm.at[row], rope_buf.at[slot], rope_sem.at[slot])

    def fetch(i):
        row, slot = order[i], lax.rem(i, ATT_BUF)
        count = blocks(order[i - i % 2 + 1])
        for blk in range(max_blk):
            @pl.when(blk < count)
            def _():
                lat_copy(row, blk, slot).start()
        rope_copy(row, slot).start()

    def land(i):
        row, slot = order[i], lax.rem(i, ATT_BUF)
        count = blocks(order[i - i % 2 + 1])
        for blk in range(max_blk):
            @pl.when(blk < count)
            def _():
                lat_copy(row, blk, slot).wait()
        rope_copy(row, slot).wait()

    small = [pltpu.make_async_copy(src, dst, in_sem.at[i]) for i, (src, dst) in enumerate(((q_hbm, q_all), (q2_hbm, q2_all), (nl_hbm, nl_out), (nr_hbm, nr_out), (wuv_hbm, wuv)))]
    for i in range(2):
        fetch(i)
    for cp in small[:4]:
        cp.start()
    for i in range(2, ATT_BUF - 2):
        fetch(i)
    small[4].start()
    for cp in small[:4]:
        cp.wait()
    nl_rows[...] = nl_out[...].astype(f32)
    own_col = lax.broadcasted_iota(jnp.int32, (heads, rows), 1)
    nt = (((1,), (1,)), ((), ()))

    def scores(row, slot, span):
        lat = lat_buf[slot, :span]
        q_lat = q_all[row]
        q2 = q2_all[row]
        q_rot = jnp.concatenate([q2[a : a + n_pair, b : b + r_dim] for a in (0, n_pair) for b in (0, r_dim)], axis=0)
        s = lax.dot_general(lat, q_lat, nt, preferred_element_type=f32).T
        s = s + jnp.dot(q_rot, rope_buf[slot, :, :span], preferred_element_type=f32)
        own = lax.dot_general(q_lat, nl_out[...], nt, preferred_element_type=f32) + lax.dot_general(q_rot, nr_out[...], nt, preferred_element_type=f32)
        own = jnp.sum(jnp.where(own_col == row, own, 0.0), axis=1, keepdims=True) * scale
        return s * scale, own

    def softmax(s, own, row, span):
        pos = lax.broadcasted_iota(jnp.int32, (heads, span), 1)
        s = jnp.where(pos < lens_ref[row], s, -jnp.inf)
        top = jnp.maximum(jnp.max(s, axis=1, keepdims=True), own)
        e = jnp.exp(s - top)
        own_e = jnp.exp(own - top)
        inv = 1.0 / (jnp.sum(e, axis=1, keepdims=True) + own_e)
        return (e * inv).astype(jnp.bfloat16), (own_e * inv).astype(jnp.bfloat16).astype(f32)

    def mixed(prob, own_p, row, slot, span):
        acc = jnp.dot(prob, lat_buf[slot, :span], preferred_element_type=f32)
        return (acc + own_p * nl_rows[pl.ds(row, 1), :]).astype(jnp.bfloat16)

    def pair_step(i, carry):
        first, second = 2 * i, 2 * i + 1

        @pl.when(second + ATT_BUF - 2 < rows)
        def _():
            fetch(first + ATT_BUF - 2)
            fetch(second + ATT_BUF - 2)

        land(first)
        land(second)
        pair = ((order[first], lax.rem(first, ATT_BUF)), (order[second], lax.rem(second, ATT_BUF)))
        count = blocks(pair[1][0])
        for num in range(1, max_blk + 1):
            @pl.when(count == num)
            def _():
                span = num * ATT_BLK
                raw = [scores(row, slot, span) for row, slot in pair]
                prob = [softmax(s, own, row, span) for (s, own), (row, _) in zip(raw, pair)]
                for (p, own_p), (row, slot) in zip(prob, pair):
                    mix[row] = mixed(p, own_p, row, slot, span)
        return carry

    lax.fori_loop(0, rows // 2, pair_step, 0)
    small[4].wait()
    v_dim = wuv.shape[2]

    def head_group(grp, carry):
        base = pl.multiple_of(grp * (heads // 2), heads // 2)
        lhs = mix[:, pl.ds(base, heads // 2), :].reshape(rows, heads // 2 * kv_dim)
        for part in range(heads // 2 // UV_HEADS):
            rhs = wuv[:, pl.ds(pl.multiple_of(base + part * UV_HEADS, UV_HEADS), UV_HEADS), :].reshape(kv_dim, UV_HEADS * v_dim)
            for h in range(UV_HEADS):
                head = part * UV_HEADS + h
                at = (head % 2) * (heads // 4) + head // 2
                out = jnp.dot(lhs[:, at * kv_dim : (at + 1) * kv_dim], rhs[:, h * v_dim : (h + 1) * v_dim], preferred_element_type=jnp.float32)
                o_ref[:, pl.ds(pl.multiple_of((base + head) * v_dim, v_dim), v_dim)] = out.astype(jnp.bfloat16)
        return carry

    lax.fori_loop(0, 2, head_group, 0)


def attention(lens, q_abs, q_pairs, new_lat, new_rope, cache_lat, rope_t, w_uv):
    rows, heads, kv_dim = q_abs.shape
    cache_len = cache_lat.shape[1]
    rope_dim = new_rope.shape[1]
    v_dim = w_uv.shape[2]
    vmem = pl.BlockSpec(memory_space=pltpu.VMEM)
    hbm = pl.BlockSpec(memory_space=pl.ANY)
    max_blk = cache_len // ATT_BLK
    return pl.pallas_call(
        attn_kernel,
        out_shape=(jax.ShapeDtypeStruct((rows, heads * v_dim), jnp.bfloat16), jax.ShapeDtypeStruct((rows, kv_dim), jnp.bfloat16), jax.ShapeDtypeStruct((rows, rope_dim), jnp.bfloat16)),
        in_specs=[pl.BlockSpec(memory_space=pltpu.SMEM)] + [hbm] * 7,
        out_specs=(vmem, vmem, vmem),
        scratch_shapes=[
            pltpu.VMEM((ATT_BUF, cache_len, kv_dim), jnp.bfloat16),
            pltpu.VMEM((ATT_BUF, rope_dim, cache_len), jnp.bfloat16),
            pltpu.VMEM((rows, heads, kv_dim), jnp.bfloat16),
            pltpu.VMEM((kv_dim, heads, v_dim), jnp.bfloat16),
            pltpu.VMEM((rows, heads, kv_dim), jnp.bfloat16),
            pltpu.VMEM((rows, heads // 2, 2 * rope_dim), jnp.bfloat16),
            pltpu.VMEM((rows, kv_dim), jnp.float32),
            pltpu.SMEM((rows,), jnp.int32),
            pltpu.SMEM((max_blk + 1,), jnp.int32),
            pltpu.SemaphoreType.DMA((ATT_BUF, max_blk)),
            pltpu.SemaphoreType.DMA((ATT_BUF,)),
            pltpu.SemaphoreType.DMA((5,)),
        ],
        compiler_params=pltpu.CompilerParams(vmem_limit_bytes=67043328),
        cost_estimate=pl.CostEstimate(flops=10**10, bytes_accessed=40 * 10**6, transcendentals=0),
        name="attention",
    )(lens, q_abs, q_pairs, new_lat, new_rope, cache_lat, rope_t, w_uv)


RING = 28
TILE_K = 2048
TILE_N = 256
RS_N = 512
GATHER_LAG = 5
DIRECT = 4


def mlp_kernel(n_dev, o_ref, x_ref, gain_ref, wo_hbm, wg_hbm, wu_hbm, wd_hbm, out_ref,
               ring, o_all, x_all, x_send, h_all, m_all, u_own, u_peer, wd_peer, acc, part, own_part, near, far, fin,
               ring_sem, pair_sem, in_sem, gat_send, gat_recv, u_sem, rs_send, rs_recv):
    rows, d_model = x_ref.shape
    heads_dim = o_ref.shape[1]
    half = d_model // 2
    ff = wg_hbm.shape[1]
    chips = n_dev // 2
    pair = 2 * rows
    total = n_dev * rows
    f32 = jnp.float32
    me = lax.axis_index("g")
    core = me % 2
    chip = me // 2
    peer = chip * 2 + (1 - core)
    right_chip = (chip + 1) % chips
    left_chip = (chip + chips - 1) % chips
    far_chip = (chip + 2) % chips
    right = right_chip * 2 + core
    left = left_chip * 2 + core
    across = far_chip * 2 + core
    col0 = pl.multiple_of(core * half, half)
    other0 = pl.multiple_of((1 - core) * half, half)

    def remote(src, dst, send, recv, dev):
        return pltpu.make_async_remote_copy(src_ref=src, dst_ref=dst, send_sem=send, recv_sem=recv, device_id={"g": dev}, device_id_type=MESH)

    wo_k = heads_dim // TILE_K
    wo_j = half // TILE_N
    n_wo = wo_j * wo_k
    gu_k = d_model // TILE_K
    gu_n = ff // TILE_N
    n_gu = gu_n * 2 * gu_k
    wd_n = half // TILE_N
    rs_n = half // RS_N
    rs_t = RS_N // TILE_N
    n_all = n_wo + n_gu + wd_n

    def ring_copy(src, slot, depth):
        return pltpu.make_async_copy(src, ring.at[slot, pl.ds(0, depth)], ring_sem.at[slot])

    def issue(t):
        slot = t % RING

        @pl.when(t < n_wo)
        def _():
            j, k = t // wo_k, t % wo_k
            ring_copy(wo_hbm.at[pl.ds(pl.multiple_of(k * TILE_K, TILE_K), TILE_K), pl.ds(pl.multiple_of(col0 + j * TILE_N, TILE_N), TILE_N)], slot, TILE_K).start()

        for mat, w_hbm in ((0, wg_hbm), (1, wu_hbm)):
            q = t - n_wo

            @pl.when((q >= 0) & (q < n_gu) & ((q // gu_k) % 2 == mat))
            def _():
                n, k = q // (2 * gu_k), q % gu_k
                ring_copy(w_hbm.at[pl.ds(pl.multiple_of(k * TILE_K, TILE_K), TILE_K), pl.ds(pl.multiple_of(n * TILE_N, TILE_N), TILE_N)], slot, TILE_K).start()

        @pl.when((t >= n_wo + n_gu) & (t < n_all))
        def _():
            n = t - n_wo - n_gu
            ring_copy(wd_hbm.at[:, pl.ds(pl.multiple_of(col0 + n * TILE_N, TILE_N), TILE_N)], slot, ff).start()

    def arrive(t, depth):
        slot = t % RING
        ring_copy(wo_hbm.at[pl.ds(0, depth), pl.ds(0, TILE_N)], slot, depth).wait()
        return slot

    my_rows = pl.ds(pl.multiple_of(core * rows, rows), rows)
    o_load = pltpu.make_async_copy(o_ref, o_all.at[my_rows], in_sem.at[0])
    x_load = pltpu.make_async_copy(x_ref.at[:, pl.ds(col0, half)], x_all.at[my_rows], in_sem.at[1])
    x_other = pltpu.make_async_copy(x_ref.at[:, pl.ds(other0, half)], x_send, in_sem.at[2])
    o_load.start()
    x_other.start()
    x_load.start()

    def first(t, carry):
        issue(t)
        return carry

    lax.fori_loop(0, RING, first, 0)

    barrier = pltpu.get_barrier_semaphore()
    for dev in (peer, left, right, across):
        pl.semaphore_signal(barrier, inc=1, device_id={"g": dev}, device_id_type=MESH)
    pl.semaphore_wait(barrier, 4)

    o_copy = remote(o_all.at[my_rows], o_all.at[my_rows], pair_sem.at[0], pair_sem.at[1], peer)
    x_copy = remote(x_send, x_all.at[my_rows], pair_sem.at[2], pair_sem.at[3], peer)
    wd_copy = remote(wd_hbm.at[:, pl.ds(other0, half)], wd_peer, pair_sem.at[4], pair_sem.at[5], peer)
    o_load.wait()
    o_copy.start()
    x_other.wait()
    x_copy.start()
    wd_copy.start()
    x_load.wait()
    o_copy.wait()
    x_copy.wait()

    def rows_of(c, lo, num):
        return pl.ds(pl.multiple_of(c * pair + lo, rows), num)

    n_send = half // TILE_N

    def block_of(s):
        return core * n_send + s

    def near_copy(s, to_right):
        region = h_all.at[block_of(s), rows_of(chip, 0, pair)]
        side = 0 if to_right else 1
        return remote(region, region, gat_send.at[side, s], gat_recv.at[side, s], right if to_right else left)

    def pass_copy(s, to_right):
        src_chip = left_chip if to_right else right_chip
        region = h_all.at[block_of(s), rows_of(src_chip, 0 if to_right else rows, rows)]
        side = 2 if to_right else 3
        return remote(region, region, gat_send.at[side, s], gat_recv.at[side, s], right if to_right else left)

    def far_copy(s):
        region = h_all.at[block_of(s), rows_of(chip, 0, pair)]
        return remote(region, region, gat_send.at[2, s], gat_recv.at[2, s], across)

    def peer_copy(s):
        region = h_all.at[block_of(s)]
        return remote(region, region, gat_send.at[4, s], gat_recv.at[4, s], peer)

    relayed = n_send - DIRECT

    def gather_step(s):
        sent = s - 1

        @pl.when((sent >= 0) & (sent < n_send))
        def _():
            near_copy(sent, True).start()
            near_copy(sent, False).start()

        @pl.when((sent >= relayed) & (sent < n_send))
        def _():
            far_copy(sent).start()

        here = s - GATHER_LAG

        @pl.when((here >= 0) & (here < n_send))
        def _():
            near_copy(here, True).wait_recv()
            near_copy(here, False).wait_recv()

        @pl.when((here >= 0) & (here < relayed))
        def _():
            pass_copy(here, True).start()
            pass_copy(here, False).start()

        done = s - 2 * GATHER_LAG + 1

        @pl.when((done >= 0) & (done < relayed))
        def _():
            pass_copy(done, True).wait_recv()
            pass_copy(done, False).wait_recv()
            peer_copy(done).start()

        @pl.when((here >= relayed) & (here < n_send))
        def _():
            far_copy(here).wait_recv()
            peer_copy(here).start()

    def wo_step(j, carry):
        gather_step(j)
        slots = [arrive(j * wo_k + k, TILE_K) for k in range(wo_k)]
        prod = jnp.zeros((pair, TILE_N), f32)
        for k in range(wo_k):
            prod = prod + jnp.dot(o_all[:, k * TILE_K : (k + 1) * TILE_K], ring[slots[k]], preferred_element_type=f32)
        xs = x_all[:, pl.ds(pl.multiple_of(j * TILE_N, TILE_N), TILE_N)].astype(f32)
        h_all[block_of(j), rows_of(chip, 0, pair), :] = (xs + prod).astype(jnp.bfloat16)
        for k in range(wo_k):
            issue(j * wo_k + k + RING)
        return carry

    lax.fori_loop(0, wo_j, wo_step, 0)

    def drain(s, carry):
        gather_step(s)
        return carry

    lax.fori_loop(wo_j, max(n_send + GATHER_LAG, relayed + 2 * GATHER_LAG - 1), drain, 0)

    def settle(s, carry):
        peer_copy(s).wait()
        for to_right in (True, False):
            near_copy(s, to_right).wait_send()

        @pl.when(s < relayed)
        def _():
            pass_copy(s, True).wait_send()
            pass_copy(s, False).wait_send()

        @pl.when(s >= relayed)
        def _():
            far_copy(s).wait_send()

        return carry

    lax.fori_loop(0, n_send, settle, 0)

    gain_rows = gain_ref[...].astype(f32)

    def norm_rows(b, carry):
        block = pl.ds(pl.multiple_of(b * 16, 16), 16)
        lanes = jnp.zeros((16, 128), f32)
        for c in range(d_model // TILE_N):
            v = h_all[c, block, :].astype(f32)
            sq = v * v
            lanes = lanes + (sq[:, :128] + sq[:, 128:])
        inv = lax.rsqrt(jnp.sum(lanes, axis=1, keepdims=True) / d_model + 1e-6)
        for c in range(0, d_model, 128):
            v = h_all[c // TILE_N, block, c % TILE_N : c % TILE_N + 128].astype(f32)
            m_all[block, c : c + 128] = (v * inv * gain_rows[c // 128 : c // 128 + 1]).astype(jnp.bfloat16)
        return carry

    lax.fori_loop(0, total // 16, norm_rows, 0)

    def u_copy(n):
        span = pl.ds(pl.multiple_of(n * TILE_N, TILE_N), TILE_N)
        return remote(u_own.at[:, span], u_peer.at[:, span], u_sem.at[0, n], u_sem.at[1, n], peer)

    def gu_step(n, carry):
        t0 = n_wo + n * 2 * gu_k
        slots = [arrive(t0 + i, TILE_K) for i in range(2 * gu_k)]
        g = jnp.zeros((total, TILE_N), f32)
        u = jnp.zeros((total, TILE_N), f32)
        for k in range(gu_k):
            g = g + jnp.dot(m_all[:, k * TILE_K : (k + 1) * TILE_K], ring[slots[k]], preferred_element_type=f32)
        for k in range(gu_k):
            u = u + jnp.dot(m_all[:, k * TILE_K : (k + 1) * TILE_K], ring[slots[gu_k + k]], preferred_element_type=f32)
        for i in range(2 * gu_k):
            issue(t0 + i + RING)
        u_own[:, pl.ds(pl.multiple_of(n * TILE_N, TILE_N), TILE_N)] = (jax.nn.silu(g) * u).astype(jnp.bfloat16)
        u_copy(n).start()
        return carry

    lax.fori_loop(0, gu_n, gu_step, 0)
    wd_copy.wait()
    for n in range(gu_n):
        u_copy(n).wait()

    def rs_near(n, to_right):
        side = 0 if to_right else 1
        c = right_chip if to_right else left_chip
        return remote(part.at[n, rows_of(c, 0, pair)], near.at[side, n], rs_send.at[side, n], rs_recv.at[side, n], right if to_right else left)

    def rs_far(n):
        return remote(part.at[n, rows_of(far_chip, 0, pair)], far.at[n], rs_send.at[2, n], rs_recv.at[2, n], across)

    def out_cols(n):
        return pl.ds(pl.multiple_of(col0 + n * RS_N, RS_N), RS_N)

    def rs_out(n):
        return remote(fin.at[n], out_ref.at[:, out_cols(n)], rs_send.at[3, n], rs_recv.at[3, n], peer)

    def down_step(n, carry):
        for i in range(rs_t):
            slot = arrive(n_wo + n_gu + n * rs_t + i, ff)
            cols = pl.ds(pl.multiple_of(n * RS_N + i * TILE_N, TILE_N), TILE_N)
            acc[...] = jnp.dot(u_own[...], ring[slot, :ff], preferred_element_type=f32) + jnp.dot(u_peer[...], wd_peer[:, cols], preferred_element_type=f32)
            part[n, :, i * TILE_N : (i + 1) * TILE_N] = acc[...].astype(jnp.bfloat16)
            own_part[n, :, i * TILE_N : (i + 1) * TILE_N] = acc[rows_of(chip, 0, pair), :]
        rs_far(n).start()
        for to_right in (True, False):
            rs_near(n, to_right).start()
        return carry

    lax.fori_loop(0, rs_n, down_step, 0)

    def final_step(n, carry):
        rs_far(n).wait_recv()
        for to_right in (True, False):
            rs_near(n, to_right).wait_recv()
        def rows_sum(side):
            blk = slice(side * rows, (side + 1) * rows)
            mlp = own_part[n, blk] + near[0, n, blk].astype(f32) + near[1, n, blk].astype(f32) + far[n, blk].astype(f32)
            resid = jnp.concatenate([h_all[block_of(n * rs_t + i), rows_of(chip, side * rows, rows), :] for i in range(rs_t)], axis=1)
            return (resid.astype(f32) + mlp).astype(jnp.bfloat16)

        low = rows_sum(0)
        high = rows_sum(1)
        out_ref[:, out_cols(n)] = jnp.where(core == 0, low, high)
        fin[n] = jnp.where(core == 0, high, low)
        rs_out(n).start()
        return carry

    lax.fori_loop(0, rs_n, final_step, 0)

    def finish(n, carry):
        rs_out(n).wait()
        rs_far(n).wait_send()
        for to_right in (True, False):
            rs_near(n, to_right).wait_send()
        return carry

    lax.fori_loop(0, rs_n, finish, 0)


def out_proj_mlp(n_dev, o, x, gain, w_o, w_gate, w_up, w_down):
    rows, d_model = x.shape
    half = d_model // 2
    ff = w_gate.shape[1]
    pair, total = 2 * rows, n_dev * rows
    bf16, f32 = jnp.bfloat16, jnp.float32
    vmem = pl.BlockSpec(memory_space=pltpu.VMEM)
    hbm = pl.BlockSpec(memory_space=pl.ANY)
    n_send, rs_n = half // TILE_N, half // RS_N
    dma = pltpu.SemaphoreType.DMA
    return pl.pallas_call(
        functools.partial(mlp_kernel, n_dev),
        out_shape=jax.ShapeDtypeStruct((rows, d_model), bf16),
        in_specs=[hbm, hbm, vmem, hbm, hbm, hbm, hbm],
        out_specs=vmem,
        scratch_shapes=[
            pltpu.VMEM((RING, TILE_K, TILE_N), bf16),
            pltpu.VMEM((pair, o.shape[1]), bf16),
            pltpu.VMEM((pair, half), bf16),
            pltpu.VMEM((rows, half), bf16),
            pltpu.VMEM((d_model // TILE_N, total, TILE_N), bf16),
            pltpu.VMEM((total, d_model), bf16),
            pltpu.VMEM((total, ff), bf16),
            pltpu.VMEM((total, ff), bf16),
            pltpu.VMEM((ff, half), bf16),
            pltpu.VMEM((total, TILE_N), f32),
            pltpu.VMEM((rs_n, total, RS_N), bf16),
            pltpu.VMEM((rs_n, pair, RS_N), f32),
            pltpu.VMEM((2, rs_n, pair, RS_N), bf16),
            pltpu.VMEM((rs_n, pair, RS_N), bf16),
            pltpu.VMEM((rs_n, rows, RS_N), bf16),
            dma((RING,)),
            dma((6,)),
            dma((3,)),
            dma((5, n_send)),
            dma((5, n_send)),
            dma((2, ff // TILE_N)),
            dma((4, rs_n)),
            dma((4, rs_n)),
        ],
        compiler_params=pltpu.CompilerParams(vmem_limit_bytes=67043328, collective_id=1, has_side_effects=True),
        cost_estimate=pl.CostEstimate(flops=2 * 10**10, bytes_accessed=116 * 10**6, transcendentals=0),
        name="out_proj_mlp",
    )(o, x, gain, w_o, w_gate, w_up, w_down)


def solution(mesh):
    row_spec = P(("rep", "g"))
    full_spec = P()
    in_specs = (row_spec, row_spec, row_spec, row_spec, full_spec, full_spec, full_spec, full_spec, full_spec, full_spec, full_spec, full_spec, full_spec, full_spec, full_spec, P(None, "g"), P(None, "g"), P("g", None))
    n_dev = mesh.shape["g"]

    def local_step(hidden, cache_lat, cache_rope, seq_lens, gain_attn, w_dq, gain_q, w_uq, w_qr, w_dkv, gain_kv, w_uk, w_uv, w_o, gain_mlp, w_gate, w_up, w_down):
        q_abs, q_pairs, lat, rope = projections(n_dev, seq_lens, hidden, gain_attn, w_dq, gain_q, w_uq, w_qr, w_dkv, gain_kv, w_uk)
        out_heads, new_lat, new_rope = attention(seq_lens, q_abs, q_pairs, lat, rope, cache_lat, jnp.swapaxes(cache_rope, 1, 2), w_uv)
        out_hidden = out_proj_mlp(n_dev, out_heads, hidden, gain_mlp.reshape(-1, 128), w_o, w_gate, w_up, w_down)
        return out_hidden, new_lat, new_rope

    return jax.shard_map(local_step, mesh=mesh, in_specs=in_specs, out_specs=(row_spec, row_spec, row_spec), check_vma=False)
```

time: 175 us -> 123 us (0.70)
  matrix products: 48.6 us -> 0 us
  Pallas kernels: 114 us -> 121 us
  local copies, waits for them, and re-layouts: 7.5 us -> 1.77 us
  other arithmetic: 4.23 us -> 0 us
    dot_general x4 -> x0, matrix products: 48.6 us -> none  [the longest x1 29.2 us: attention_rows(): jnp.einsum('bhn,chn->bhc', q_nope, w_uk, preferred_element_type=jnp.float32)]
    pallas_call x1 -> x2, Pallas kernels: 40.8 us -> 52.9 us  [the longest x1 32.2 us: attention(): pl.pallas_call(attn_kernel, out_shape=(jax.ShapeDtypeStruct((rows, heads...]
    pallas_call x1, Pallas kernels: 73.2 us -> 67.9 us  [out_proj_mlp(): pl.pallas_call(functools.partial(mlp_kernel, n_dev), out_shape=jax.ShapeD...]
    unnamed x25 -> x1, local copies, waits for them, and re-layouts: 5.28 us -> 1.77 us
where the time goes in v1:
time: 123 us
  Pallas kernels  121 us (98%)
  local copies, waits for them, and re-layouts  1.77 us (1%)
    pallas_call x1, Pallas kernels, out_proj_mlp(): pl.pallas_call(functools.partial(mlp_kernel, n_dev), out_shape=jax.ShapeD...  67.9 us
    pallas_call x1, Pallas kernels, attention(): pl.pallas_call(attn_kernel, out_shape=(jax.ShapeDtypeStruct((rows, heads...  32.2 us
    pallas_call x1, Pallas kernels, projections(): pl.pallas_call(functools.partial(proj_kernel, n_dev), out_shape=(jax.Shap...  20.7 us

profile of v1, /device:TPU:113, one launch (start us, length us, event | category | flops | bytes accessed | tf_op | source)
XLA Modules:
  0.0 123.3 jit_solution(17265912973192119312)
XLA Ops:
  0.6 20.7 %projections.1 = (bf16[32,64,512]{2,1,0:T(8,128)(2,1)}, bf16[32,32,128]{2,1,0:T(8,128)(2,1)}, bf16[32,512]{1,0:T(8,128)(2,1)}, bf16[32,64]{1,0:T(8,128)(2,1)}) custom-call(s32[32]{0:T(128)} %lens_ref.3, bf16[32,6144]{1,0:T(8,128)(2,1)} %x_ref.3, f32[1,128]{1,0:T(1,128)} %constant.2.clone.freq_ref, bf16[48,128]{1,0:T(8,128)(2,1)} %bitcast.12, ...), custom_call_target="tpu_custom_call" | custom-call | flops 5000000000 | bytes 40000000 | tf_op jit(solution)/shard_map/projections/pallas_call | solution.py:186
  21.3 32.2 %attention.1 = (bf16[32,8192]{1,0:T(8,128)(2,1)}, bf16[32,512]{1,0:T(8,128)(2,1)}, bf16[32,64]{1,0:T(8,128)(2,1)}) custom-call(s32[32]{0:T(128)} %lens_ref.3, bf16[32,64,512]{2,1,0:T(8,128)(2,1)} %get-tuple-element.10.q_hbm, bf16[32,32,128]{2,1,0:T(8,128)(2,1)} %get-tuple-element.11.q2_hbm, bf16[32,512]{1,0:T(8,128)(2,1)} %get-tuple-element.12.nl_hbm, ...), custom_call_target="tpu_custom_call" | custom-call | flops 10000000000 | bytes 40000000 | tf_op jit(solution)/shard_map/attention/pallas_call | solution.py:367
  53.6 67.9 %out_proj_mlp.1 = bf16[32,6144]{1,0:T(8,128)(2,1)} custom-call(bf16[32,8192]{1,0:T(8,128)(2,1)} %get-tuple-element.14.o_ref, bf16[32,6144]{1,0:T(8,128)(2,1)} %x_ref.3, bf16[48,128]{1,0:T(8,128)(2,1)} %bitcast.13, bf16[8192,6144]{1,0:T(8,128)(2,1)} %wo_hbm.1, bf16[6144,1536]{1,0:T(8,128)(2,1)} %wg_hbm.1, bf16[6144,1536]{1,0:T(8,128)(2,1)} %wu_hbm.1, ...), custom_call_target="tpu_custom_call" | custom-call | flops 20000000000 | bytes 116000000 | tf_op jit(solution)/shard_map/out_proj_mlp/pallas_call | solution.py:710
  121.5 1.8 %copy.23 = bf16[32,6144]{1,0:T(8,128)(2,1)} copy(bf16[32,6144]{1,0:T(8,128)(2,1)} %out_proj_mlp.1) | data formatting | bytes 786432

commit v2 on v1

--- a/solution.py
+++ b/solution.py
@@ -13,9 +13,9 @@
 DQ_K = 1024
 
 
-def proj_kernel(n_dev, lens_ref, x_ref, freq_ref, ga_ref, gq_ref, gkv_ref, wdq_hbm, wdkv_hbm, wuq_hbm, wqr_hbm, wuk_hbm,
+def proj_kernel(n_dev, lens_ref, x_hbm, freq_ref, ga_ref, gq_ref, gkv_ref, wdq_hbm, wdkv_hbm, wuq_hbm, wqr_hbm, wuk_hbm,
                 q_out, q2_out, nl_out, nr_out,
-                wdq, wdkv, wuq, wqr, wuk, a_all, t_all, c_all, ang, kv_buf, kv_send, qh, qx, rh, rx,
+                x_ref, wdq, wdkv, wuq, wqr, wuk, a_all, t_all, c_all, ang, kv_buf, kv_send, qh, qx, rh, rx,
                 w_sem, x_sem, q_sem):
     rows, d_model = x_ref.shape
     f32, bf16 = jnp.float32, jnp.bfloat16
@@ -49,8 +49,12 @@
     qr_rows = wqr.shape[0]
     qr_load = pltpu.make_async_copy(wqr_hbm.at[pl.ds(pl.multiple_of(core * qr_rows, qr_rows), qr_rows)], wqr, w_sem.at[n_dq + 1 + 2 * n_grp])
     loads.append(qr_load)
+    x_load = pltpu.make_async_copy(x_hbm, x_ref, w_sem.at[n_dq + 2 + 2 * n_grp])
+    x_load.start()
     for cp in loads:
         cp.start()
+    barrier = pltpu.get_barrier_semaphore()
+    pl.semaphore_signal(barrier, inc=1, device_id={"g": peer}, device_id_type=MESH)
 
     def remote(src, dst, i):
         return pltpu.make_async_remote_copy(src_ref=src, dst_ref=dst, send_sem=x_sem.at[0, i], recv_sem=x_sem.at[1, i], device_id={"g": peer}, device_id_type=MESH)
@@ -60,6 +64,7 @@
     for r in range(rows):
         pos = jnp.where(row_id == r, lens_ref[r], pos)
     ang[my_rows, :] = pos.astype(f32) * freq_ref[...]
+    x_load.wait()
     lanes = jnp.zeros((rows, 128), f32)
     for c in range(0, d_model, 512):
         v = x_ref[:, c : c + 512].astype(f32)
@@ -70,8 +75,6 @@
     for c in range(0, d_model, 128):
         v = x_ref[:, c : c + 128].astype(f32)
         a_all[my_rows, c : c + 128] = (v * inv * ga_rows[c // 128 : c // 128 + 1]).astype(bf16)
-    barrier = pltpu.get_barrier_semaphore()
-    pl.semaphore_signal(barrier, inc=1, device_id={"g": peer}, device_id_type=MESH)
     pl.semaphore_wait(barrier, 1)
     a_copy = remote(a_all.at[my_rows], a_all.at[my_rows], 0)
     ang_copy = remote(ang.at[my_rows], ang.at[my_rows], 1)
@@ -191,9 +194,10 @@
             jax.ShapeDtypeStruct((rows, kv_dim), bf16),
             jax.ShapeDtypeStruct((rows, rope_dim), bf16),
         ),
-        in_specs=[pl.BlockSpec(memory_space=pltpu.SMEM), vmem, vmem, vmem, vmem, vmem, hbm, hbm, hbm, hbm, hbm],
+        in_specs=[pl.BlockSpec(memory_space=pltpu.SMEM), hbm, vmem, vmem, vmem, vmem, hbm, hbm, hbm, hbm, hbm],
         out_specs=(vmem, vmem, vmem, vmem),
         scratch_shapes=[
+            pltpu.VMEM((rows, d_model), bf16),
             pltpu.VMEM((d_model, q_dim // 2), bf16),
             pltpu.VMEM((kv_cols, d_model), bf16),
             pltpu.VMEM((n_grp, q_dim, HEAD_GRP, n_dim), bf16),
@@ -209,7 +213,7 @@
             pltpu.VMEM((my_heads, rows, kv_dim), bf16),
             pltpu.VMEM((my_heads // 2, pair, 128), bf16),
             pltpu.VMEM((my_heads // 2, rows, 128), bf16),
-            dma((d_model // DQ_K + 2 + 2 * n_grp,)),
+            dma((d_model // DQ_K + 3 + 2 * n_grp,)),
             dma((2, 5)),
             dma((2, 2 * n_grp)),
         ],
@@ -220,7 +224,8 @@
 
 
 ATT_BLK = 256
-ATT_BUF = 8
+ATT_BUF = 12
+ROWS_STEP = 4
 UV_HEADS = 16
 
 
@@ -261,7 +266,7 @@
 
     def fetch(i):
         row, slot = order[i], lax.rem(i, ATT_BUF)
-        count = blocks(order[i - i % 2 + 1])
+        count = blocks(order[i - i % ROWS_STEP + ROWS_STEP - 1])
         for blk in range(max_blk):
             @pl.when(blk < count)
             def _():
@@ -270,7 +275,7 @@
 
     def land(i):
         row, slot = order[i], lax.rem(i, ATT_BUF)
-        count = blocks(order[i - i % 2 + 1])
+        count = blocks(order[i - i % ROWS_STEP + ROWS_STEP - 1])
         for blk in range(max_blk):
             @pl.when(blk < count)
             def _():
@@ -282,7 +287,7 @@
         fetch(i)
     for cp in small[:4]:
         cp.start()
-    for i in range(2, ATT_BUF - 2):
+    for i in range(2, ATT_BUF - ROWS_STEP):
         fetch(i)
     small[4].start()
     for cp in small[:4]:
@@ -316,17 +321,17 @@
         return (acc + own_p * nl_rows[pl.ds(row, 1), :]).astype(jnp.bfloat16)
 
     def pair_step(i, carry):
-        first, second = 2 * i, 2 * i + 1
-
-        @pl.when(second + ATT_BUF - 2 < rows)
-        def _():
-            fetch(first + ATT_BUF - 2)
-            fetch(second + ATT_BUF - 2)
-
-        land(first)
-        land(second)
-        pair = ((order[first], lax.rem(first, ATT_BUF)), (order[second], lax.rem(second, ATT_BUF)))
-        count = blocks(pair[1][0])
+        first = ROWS_STEP * i
+
+        @pl.when(first + ATT_BUF < rows + ROWS_STEP)
+        def _():
+            for r in range(ROWS_STEP):
+                fetch(first + ATT_BUF - ROWS_STEP + r)
+
+        for r in range(ROWS_STEP):
+            land(first + r)
+        pair = [(order[first + r], lax.rem(first + r, ATT_BUF)) for r in range(ROWS_STEP)]
+        count = blocks(pair[-1][0])
         for num in range(1, max_blk + 1):
             @pl.when(count == num)
             def _():
@@ -337,7 +342,7 @@
                     mix[row] = mixed(p, own_p, row, slot, span)
         return carry
 
-    lax.fori_loop(0, rows // 2, pair_step, 0)
+    lax.fori_loop(0, rows // ROWS_STEP, pair_step, 0)
     small[4].wait()
     v_dim = wuv.shape[2]
 
@@ -392,9 +397,9 @@
 RING = 28
 TILE_K = 2048
 TILE_N = 256
-RS_N = 512
+RS_N = 256
 GATHER_LAG = 5
-DIRECT = 4
+DIRECT = 2
 
 
 def mlp_kernel(n_dev, o_ref, x_ref, gain_ref, wo_hbm, wg_hbm, wu_hbm, wd_hbm, out_ref,
@@ -472,21 +477,22 @@
     x_other.start()
     x_load.start()
 
-    def first(t, carry):
-        issue(t)
-        return carry
-
-    lax.fori_loop(0, RING, first, 0)
-
     barrier = pltpu.get_barrier_semaphore()
     for dev in (peer, left, right, across):
         pl.semaphore_signal(barrier, inc=1, device_id={"g": dev}, device_id_type=MESH)
-    pl.semaphore_wait(barrier, 4)
+
+    def first(t, carry):
+        issue(t)
+        return carry
+
+    lax.fori_loop(0, RING, first, 0)
+
 
     o_copy = remote(o_all.at[my_rows], o_all.at[my_rows], pair_sem.at[0], pair_sem.at[1], peer)
     x_copy = remote(x_send, x_all.at[my_rows], pair_sem.at[2], pair_sem.at[3], peer)
     wd_copy = remote(wd_hbm.at[:, pl.ds(other0, half)], wd_peer, pair_sem.at[4], pair_sem.at[5], peer)
     o_load.wait()
+    pl.semaphore_wait(barrier, 4)
     o_copy.start()
     x_other.wait()
     x_copy.start()

time: 123 us -> 118 us (0.959)
  Pallas kernels: 121 us -> 115 us
    pallas_call x1, Pallas kernels: 32.2 us -> 28.7 us  [attention(): pl.pallas_call(attn_kernel, out_shape=(jax.ShapeDtypeStruct((rows, heads...]
    pallas_call x1, Pallas kernels: 67.9 us -> 65.7 us  [out_proj_mlp(): pl.pallas_call(functools.partial(mlp_kernel, n_dev), out_shape=jax.ShapeD...]
where the time goes in v2:
time: 118 us; the launch traced here: 117 us
  Pallas kernels  115 us (97%)
  local copies, waits for them, and re-layouts  1.77 us (2%)
    pallas_call x1, Pallas kernels, out_proj_mlp(): pl.pallas_call(functools.partial(mlp_kernel, n_dev), out_shape=jax.ShapeD...  65.7 us
    pallas_call x1, Pallas kernels, attention(): pl.pallas_call(attn_kernel, out_shape=(jax.ShapeDtypeStruct((rows, heads...  28.7 us
    pallas_call x1, Pallas kernels, projections(): pl.pallas_call(functools.partial(proj_kernel, n_dev), out_shape=(jax.Shap...  20.6 us

profile of v2, /device:TPU:113, one launch (start us, length us, event | category | flops | bytes accessed | tf_op | source)
XLA Modules:
  0.0 117.5 jit_solution(14603472118299071815)
XLA Ops:
  0.6 20.6 %projections.1 = (bf16[32,64,512]{2,1,0:T(8,128)(2,1)}, bf16[32,32,128]{2,1,0:T(8,128)(2,1)}, bf16[32,512]{1,0:T(8,128)(2,1)}, bf16[32,64]{1,0:T(8,128)(2,1)}) custom-call(s32[32]{0:T(128)} %lens_ref.3, bf16[32,6144]{1,0:T(8,128)(2,1)} %x_ref.1, f32[1,128]{1,0:T(1,128)} %constant.2.clone.freq_ref, bf16[48,128]{1,0:T(8,128)(2,1)} %bitcast.12, ...), custom_call_target="tpu_custom_call" | custom-call | flops 5000000000 | bytes 40000000 | tf_op jit(solution)/shard_map/projections/pallas_call | solution.py:189
  21.2 28.7 %attention.1 = (bf16[32,8192]{1,0:T(8,128)(2,1)}, bf16[32,512]{1,0:T(8,128)(2,1)}, bf16[32,64]{1,0:T(8,128)(2,1)}) custom-call(s32[32]{0:T(128)} %lens_ref.3, bf16[32,64,512]{2,1,0:T(8,128)(2,1)} %get-tuple-element.10.q_hbm, bf16[32,32,128]{2,1,0:T(8,128)(2,1)} %get-tuple-element.11.q2_hbm, bf16[32,512]{1,0:T(8,128)(2,1)} %get-tuple-element.12.nl_hbm, ...), custom_call_target="tpu_custom_call" | custom-call | flops 10000000000 | bytes 40000000 | tf_op jit(solution)/shard_map/attention/pallas_call | solution.py:372
  50.0 65.7 %out_proj_mlp.1 = bf16[32,6144]{1,0:T(8,128)(2,1)} custom-call(bf16[32,8192]{1,0:T(8,128)(2,1)} %get-tuple-element.14.o_ref, bf16[32,6144]{1,0:T(8,128)(2,1)} %x_ref.1, bf16[48,128]{1,0:T(8,128)(2,1)} %bitcast.13, bf16[8192,6144]{1,0:T(8,128)(2,1)} %wo_hbm.1, bf16[6144,1536]{1,0:T(8,128)(2,1)} %wg_hbm.1, bf16[6144,1536]{1,0:T(8,128)(2,1)} %wu_hbm.1, ...), custom_call_target="tpu_custom_call" | custom-call | flops 20000000000 | bytes 116000000 | tf_op jit(solution)/shard_map/out_proj_mlp/pallas_call | solution.py:716
  115.7 1.8 %copy.23 = bf16[32,6144]{1,0:T(8,128)(2,1)} copy(bf16[32,6144]{1,0:T(8,128)(2,1)} %out_proj_mlp.1) | data formatting | bytes 786432

commit v3 on v2

--- a/solution.py
+++ b/solution.py
@@ -14,9 +14,9 @@
 
 
 def proj_kernel(n_dev, lens_ref, x_hbm, freq_ref, ga_ref, gq_ref, gkv_ref, wdq_hbm, wdkv_hbm, wuq_hbm, wqr_hbm, wuk_hbm,
-                q_out, q2_out, nl_out, nr_out,
-                x_ref, wdq, wdkv, wuq, wqr, wuk, a_all, t_all, c_all, ang, kv_buf, kv_send, qh, qx, rh, rx,
-                w_sem, x_sem, q_sem):
+                q_hbm, q2_out, nl_out, nr_out,
+                q_out, x_ref, wdq, wdkv, wuq, wqr, wuk, a_all, t_all, c_all, ang, kv_buf, kv_send, qh, qx, rh, rx,
+                w_sem, x_sem, q_sem, out_sem):
     rows, d_model = x_ref.shape
     f32, bf16 = jnp.float32, jnp.bfloat16
     nt = (((1,), (1,)), ((), ()))
@@ -159,14 +159,22 @@
     other0 = (1 - core) * my_heads
     for p in range(0, my_heads, 16):
         q_out[:, pl.ds(pl.multiple_of(own0 + p, 16), 16), :] = jnp.swapaxes(qh[p : p + 16, my_rows, :], 0, 1)
+    def q_store(first, i):
+        at = pl.ds(pl.multiple_of(first, my_heads), my_heads)
+        return pltpu.make_async_copy(q_out.at[:, at], q_hbm.at[:, at], out_sem.at[i])
+
+    q_store(own0, 0).start()
     for cp in q_copies:
         cp.wait()
     for p in range(0, my_heads, 16):
         q_out[:, pl.ds(pl.multiple_of(other0 + p, 16), 16), :] = jnp.swapaxes(qx[p : p + 16], 0, 1)
+    q_store(other0, 1).start()
     n_pair = my_heads // 2
     q2_out[:, pl.ds(pl.multiple_of(core * n_pair, n_pair), n_pair), :] = jnp.swapaxes(rh[:, my_rows, :], 0, 1)
     r_copy.wait()
     q2_out[:, pl.ds(pl.multiple_of((1 - core) * n_pair, n_pair), n_pair), :] = jnp.swapaxes(rx[...], 0, 1)
+    q_store(own0, 0).wait()
+    q_store(other0, 1).wait()
 
 
 def projections(n_dev, lens, x, gain_attn, w_dq, gain_q, w_uq, w_qr, w_dkv, gain_kv, w_uk):
@@ -195,8 +203,9 @@
             jax.ShapeDtypeStruct((rows, rope_dim), bf16),
         ),
         in_specs=[pl.BlockSpec(memory_space=pltpu.SMEM), hbm, vmem, vmem, vmem, vmem, hbm, hbm, hbm, hbm, hbm],
-        out_specs=(vmem, vmem, vmem, vmem),
+        out_specs=(hbm, vmem, vmem, vmem),
         scratch_shapes=[
+            pltpu.VMEM((rows, n_heads, kv_dim), bf16),
             pltpu.VMEM((rows, d_model), bf16),
             pltpu.VMEM((d_model, q_dim // 2), bf16),
             pltpu.VMEM((kv_cols, d_model), bf16),
@@ -216,6 +225,7 @@
             dma((d_model // DQ_K + 3 + 2 * n_grp,)),
             dma((2, 5)),
             dma((2, 2 * n_grp)),
+            dma((2,)),
         ],
         compiler_params=pltpu.CompilerParams(vmem_limit_bytes=67043328, collective_id=0, has_side_effects=True),
         cost_estimate=pl.CostEstimate(flops=5 * 10**9, bytes_accessed=40 * 10**6, transcendentals=0),
@@ -242,6 +252,10 @@
     def blocks(row):
         return (lens_ref[row] + ATT_BLK - 1) // ATT_BLK
 
+    small = [pltpu.make_async_copy(src, dst, in_sem.at[i]) for i, (src, dst) in enumerate(((q_hbm, q_all), (q2_hbm, q2_all), (nl_hbm, nl_out), (nr_hbm, nr_out), (wuv_hbm, wuv)))]
+    for cp in small[:4]:
+        cp.start()
+
     start = jnp.int32(0)
     for num in range(1, max_blk + 1):
         fill[num] = start
@@ -282,11 +296,8 @@
                 lat_copy(row, blk, slot).wait()
         rope_copy(row, slot).wait()
 
-    small = [pltpu.make_async_copy(src, dst, in_sem.at[i]) for i, (src, dst) in enumerate(((q_hbm, q_all), (q2_hbm, q2_all), (nl_hbm, nl_out), (nr_hbm, nr_out), (wuv_hbm, wuv)))]
     for i in range(2):
         fetch(i)
-    for cp in small[:4]:
-        cp.start()
     for i in range(2, ATT_BUF - ROWS_STEP):
         fetch(i)
     small[4].start()

time: 118 us -> 117 us (level)
    pallas_call x1, Pallas kernels: 28.7 us -> 27.5 us  [attention(): pl.pallas_call(attn_kernel, out_shape=(jax.ShapeDtypeStruct((rows, heads...]
where the time goes in v3:
time: 117 us
  Pallas kernels  114 us (97%)
  local copies, waits for them, and re-layouts  1.77 us (2%)
    pallas_call x1, Pallas kernels, out_proj_mlp(): pl.pallas_call(functools.partial(mlp_kernel, n_dev), out_shape=jax.ShapeD...  66.6 us
    pallas_call x1, Pallas kernels, attention(): pl.pallas_call(attn_kernel, out_shape=(jax.ShapeDtypeStruct((rows, heads...  27.5 us
    pallas_call x1, Pallas kernels, projections(): pl.pallas_call(functools.partial(proj_kernel, n_dev), out_shape=(jax.Shap...  20.3 us

profile of v3, /device:TPU:113, one launch (start us, length us, event | category | flops | bytes accessed | tf_op | source)
XLA Modules:
  0.0 116.9 jit_solution(18243863655258871773)
XLA Ops:
  0.6 20.3 %projections.1 = (bf16[32,64,512]{2,1,0:T(8,128)(2,1)}, bf16[32,32,128]{2,1,0:T(8,128)(2,1)}, bf16[32,512]{1,0:T(8,128)(2,1)}, bf16[32,64]{1,0:T(8,128)(2,1)}) custom-call(s32[32]{0:T(128)} %lens_ref.3, bf16[32,6144]{1,0:T(8,128)(2,1)} %x_ref.1, f32[1,128]{1,0:T(1,128)} %constant.2.clone.freq_ref, bf16[48,128]{1,0:T(8,128)(2,1)} %bitcast.12, ...), custom_call_target="tpu_custom_call" | custom-call | flops 5000000000 | bytes 40000000 | tf_op jit(solution)/shard_map/projections/pallas_call | solution.py:197
  21.0 27.5 %attention.1 = (bf16[32,8192]{1,0:T(8,128)(2,1)}, bf16[32,512]{1,0:T(8,128)(2,1)}, bf16[32,64]{1,0:T(8,128)(2,1)}) custom-call(s32[32]{0:T(128)} %lens_ref.3, bf16[32,64,512]{2,1,0:T(8,128)(2,1)} %get-tuple-element.10.q_hbm, bf16[32,32,128]{2,1,0:T(8,128)(2,1)} %get-tuple-element.11.q2_hbm, bf16[32,512]{1,0:T(8,128)(2,1)} %get-tuple-element.12.nl_hbm, ...), custom_call_target="tpu_custom_call" | custom-call | flops 10000000000 | bytes 40000000 | tf_op jit(solution)/shard_map/attention/pallas_call | solution.py:383
  48.5 66.6 %out_proj_mlp.1 = bf16[32,6144]{1,0:T(8,128)(2,1)} custom-call(bf16[32,8192]{1,0:T(8,128)(2,1)} %get-tuple-element.14.o_ref, bf16[32,6144]{1,0:T(8,128)(2,1)} %x_ref.1, bf16[48,128]{1,0:T(8,128)(2,1)} %bitcast.13, bf16[8192,6144]{1,0:T(8,128)(2,1)} %wo_hbm.1, bf16[6144,1536]{1,0:T(8,128)(2,1)} %wg_hbm.1, bf16[6144,1536]{1,0:T(8,128)(2,1)} %wu_hbm.1, ...), custom_call_target="tpu_custom_call" | custom-call | flops 20000000000 | bytes 116000000 | tf_op jit(solution)/shard_map/out_proj_mlp/pallas_call | solution.py:727
  115.1 1.8 %copy.23 = bf16[32,6144]{1,0:T(8,128)(2,1)} copy(bf16[32,6144]{1,0:T(8,128)(2,1)} %out_proj_mlp.1) | data formatting | bytes 786432
